TPU v7x, 1024 devices: a whole 4x8x16 slice. The times are simulated.
1024 devices in a mesh: slab: 2 (over core), py: 16 (over z), pz: 32 (over x, y).
Axes of the slice: x: 4, y: 8, z: 16, core: 2. Of those that a mesh axis runs over, the one named last changes fastest.
Arguments:
- start_vector: float32 [256, 512, 256], P('pz', 'py', 'slab'), may hold values from -6 to 6
- potential: float32 [256, 512, 256], P('pz', 'py', 'slab'), may hold values from 0.5 to 4
Outputs:
- krylov_basis: float32 [6, 256, 512, 256], P(None, 'pz', 'py', 'slab')
- tridiagonal: float32 [2, 5], replicated
All inputs are finite; a program needn't handle non-finite values.
Results may differ from a plain program's by a relative error of at most 0.00012.
Values sent between devices are 32-bit elements; how exact they have to be, the bound alone decides.
No kernel may reach another device: no remote copies, remote signals or barrier semaphores. Data moves between devices by JAX's collectives and lax.ppermute only.
A program may use at most 32 MiB of HBM per device.

v0:
```python
import jax
import jax.numpy as jnp
from jax import lax
from jax.sharding import PartitionSpec as P

ITERS = 5


EPSILON = 1e-06


def extended(value, sides, width):
    edges = {}
    for axis, dim in sides:
        peers, length = (lax.axis_size(axis), value.shape[dim])
        up = [(i, (i + 1) % peers) for i in range(peers - 1)]
        last = lax.slice_in_dim(value, length - width, length, axis=dim)
        first = lax.slice_in_dim(value, 0, width, axis=dim)
        edges[dim] = (
            lax.ppermute(last, axis, up),
            lax.ppermute(first, axis, [(b, a) for a, b in up]),
        )
    done = []
    for _, dim in sides:
        low, high = edges[dim]
        around = [(width, width) if d in done else (0, 0) for d in range(value.ndim)]
        value = jnp.concatenate([jnp.pad(low, around), value, jnp.pad(high, around)], axis=dim)
        done.append(dim)
    return value


def sent_to_all(value, axis):
    peers = lax.axis_size(axis)
    return lax.all_to_all(
        jnp.broadcast_to(value[None], (peers, *value.shape)), axis, 0, 0, tiled=True
    )


def of_everyone(value, axis):
    return sent_to_all(value, axis).sum(axis=0)


def apply_hamiltonian(field, potential):
    padded = extended(field, (("slab", 2), ("py", 1), ("pz", 0)), 1)
    beside = padded[2:, 1:-1, 1:-1] + padded[:-2, 1:-1, 1:-1]
    beside = beside + padded[1:-1, 2:, 1:-1] + padded[1:-1, :-2, 1:-1]
    beside = beside + padded[1:-1, 1:-1, 2:] + padded[1:-1, 1:-1, :-2]
    return (6.0 + potential) * field - beside


def reduce_all(partials):
    inner = of_everyone(partials, "pz")
    return of_everyone(inner, ("slab", "py"))


def project(active, image):
    return jnp.einsum("kzyx,zyx->k", active, image, precision=lax.Precision.HIGHEST)


def remove(image, coeffs, active):
    return image - jnp.einsum("k,kzyx->zyx", coeffs, active, precision=lax.Precision.HIGHEST)


def shards(start_vector, potential):
    cell_count = (
        start_vector.size * lax.axis_size("slab") * lax.axis_size("py") * lax.axis_size("pz")
    )
    per_cell = jnp.float32(1.0 / cell_count)
    start_norm = reduce_all(jnp.sum(start_vector * start_vector).reshape(1))[0] * per_cell
    vectors = [start_vector / jnp.sqrt(start_norm + EPSILON)]
    alphas = []
    beta_list = []
    for iteration in range(ITERS):
        image = apply_hamiltonian(vectors[-1], potential)
        active = jnp.stack(vectors)
        first_coeff = reduce_all(project(active, image)) * per_cell
        image = remove(image, first_coeff, active)
        local_second = project(active, image)
        summed = (
            reduce_all(jnp.concatenate([local_second, jnp.sum(image * image).reshape(1)]))
            * per_cell
        )
        second_coeff = summed[:-1]
        image = remove(image, second_coeff, active)
        square_mean = summed[-1] - jnp.sum(second_coeff * second_coeff)
        beta_value = jnp.sqrt(square_mean + EPSILON)
        alphas.append(first_coeff[iteration] + second_coeff[iteration])
        beta_list.append(beta_value)
        vectors.append(image / beta_value)
    return (jnp.stack(vectors), jnp.stack([jnp.stack(alphas), jnp.stack(beta_list)]))


def solution(mesh):
    in_specs = (P("pz", "py", "slab"), P("pz", "py", "slab"))
    out_specs = (P(None, "pz", "py", "slab"), P())
    return jax.shard_map(shards, mesh=mesh, in_specs=in_specs, out_specs=out_specs, check_vma=False)
```

profile of v0, /device:TPU:1, one launch (start us, length us, event | category | flops | bytes accessed | tf_op | source)
XLA Modules:
  0.0 503.4 jit_solution(1672057386483583725)
XLA Ops:
  2.9 19.0 %all_to_all.132 = f32[32,1,1]{2,1,0:T(1,128)S(1)} all-to-all(f32[32,1,1]{2,1,0:T(1,128)S(1)} %broadcast_in_dim.44), channel_id=1, replica_groups=mesh['slab'=2,'py'=16,'pz'=32] {'pz'}, dimensions={0} | all-to-all | bytes 256 | tf_op jit(solution)/shard_map/all_to_all | solution.py:34
  23.2 32.8 %all_to_all.133 = f32[32,1,1]{2,1,0:T(1,128)S(1)} all-to-all(f32[32,1,1]{2,1,0:T(1,128)S(1)} %broadcast_in_dim.45), channel_id=1, replica_groups=mesh['slab'=2,'py'=16,'pz'=32] {'slab','py'}, dimensions={0} | all-to-all | bytes 256 | tf_op jit(solution)/shard_map/all_to_all | solution.py:34
  64.0 4.1 collective-permute-start.5
  76.5 13.2 %all_to_all.134 = f32[32,1,1]{2,1,0:T(1,128)S(1)} all-to-all(f32[32,1,1]{2,1,0:T(1,128)S(1)} %broadcast_in_dim.46), channel_id=1, replica_groups=mesh['slab'=2,'py'=16,'pz'=32] {'pz'}, dimensions={0} | all-to-all | bytes 256 | tf_op jit(solution)/shard_map/all_to_all | solution.py:34
  91.0 16.9 %all_to_all.135 = f32[32,1,1]{2,1,0:T(1,128)S(1)} all-to-all(f32[32,1,1]{2,1,0:T(1,128)S(1)} %broadcast_in_dim.47), channel_id=1, replica_groups=mesh['slab'=2,'py'=16,'pz'=32] {'slab','py'}, dimensions={0} | all-to-all | bytes 256 | tf_op jit(solution)/shard_map/all_to_all | solution.py:34
  111.8 11.6 %all_to_all.136 = f32[32,1,2]{2,1,0:T(1,128)S(1)} all-to-all(f32[32,1,2]{2,1,0:T(1,128)S(1)} %broadcast_in_dim.48), channel_id=1, replica_groups=mesh['slab'=2,'py'=16,'pz'=32] {'pz'}, dimensions={0} | all-to-all | bytes 512 | tf_op jit(solution)/shard_map/all_to_all | solution.py:34
  123.5 16.2 %all_to_all.137 = f32[32,1,2]{2,1,0:T(1,128)S(1)} all-to-all(f32[32,1,2]{2,1,0:T(1,128)S(1)} %broadcast_in_dim.49), channel_id=1, replica_groups=mesh['slab'=2,'py'=16,'pz'=32] {'slab','py'}, dimensions={0} | all-to-all | bytes 512 | tf_op jit(solution)/shard_map/all_to_all | solution.py:34
  149.8 4.0 collective-permute-start.11
  163.2 13.2 %all_to_all.138 = f32[32,1,2]{2,1,0:T(1,128)S(1)} all-to-all(f32[32,1,2]{2,1,0:T(1,128)S(1)} %broadcast_in_dim.50), channel_id=1, replica_groups=mesh['slab'=2,'py'=16,'pz'=32] {'pz'}, dimensions={0} | all-to-all | bytes 512 | tf_op jit(solution)/shard_map/all_to_all | solution.py:34
  176.5 16.9 %all_to_all.139 = f32[32,1,2]{2,1,0:T(1,128)S(1)} all-to-all(f32[32,1,2]{2,1,0:T(1,128)S(1)} %broadcast_in_dim.51), channel_id=1, replica_groups=mesh['slab'=2,'py'=16,'pz'=32] {'slab','py'}, dimensions={0} | all-to-all | bytes 512 | tf_op jit(solution)/shard_map/all_to_all | solution.py:34
  198.3 11.6 %all_to_all.140 = f32[32,1,3]{2,1,0:T(1,128)S(1)} all-to-all(f32[32,1,3]{2,1,0:T(1,128)S(1)} %broadcast_in_dim.52), channel_id=1, replica_groups=mesh['slab'=2,'py'=16,'pz'=32] {'pz'}, dimensions={0} | all-to-all | bytes 768 | tf_op jit(solution)/shard_map/all_to_all | solution.py:34
  210.1 16.4 %all_to_all.141 = f32[32,1,3]{2,1,0:T(1,128)S(1)} all-to-all(f32[32,1,3]{2,1,0:T(1,128)S(1)} %broadcast_in_dim.53), channel_id=1, replica_groups=mesh['slab'=2,'py'=16,'pz'=32] {'slab','py'}, dimensions={0} | all-to-all | bytes 768 | tf_op jit(solution)/shard_map/all_to_all | solution.py:34
  236.8 4.0 collective-permute-start.17
  250.2 13.2 %all_to_all.142 = f32[32,1,3]{2,1,0:T(1,128)S(1)} all-to-all(f32[32,1,3]{2,1,0:T(1,128)S(1)} %broadcast_in_dim.54), channel_id=1, replica_groups=mesh['slab'=2,'py'=16,'pz'=32] {'pz'}, dimensions={0} | all-to-all | bytes 768 | tf_op jit(solution)/shard_map/all_to_all | solution.py:34
  263.5 16.9 %all_to_all.143 = f32[32,1,3]{2,1,0:T(1,128)S(1)} all-to-all(f32[32,1,3]{2,1,0:T(1,128)S(1)} %broadcast_in_dim.55), channel_id=1, replica_groups=mesh['slab'=2,'py'=16,'pz'=32] {'slab','py'}, dimensions={0} | all-to-all | bytes 768 | tf_op jit(solution)/shard_map/all_to_all | solution.py:34
  285.3 11.6 %all_to_all.144 = f32[32,1,4]{2,1,0:T(1,128)S(1)} all-to-all(f32[32,1,4]{2,1,0:T(1,128)S(1)} %broadcast_in_dim.56), channel_id=1, replica_groups=mesh['slab'=2,'py'=16,'pz'=32] {'pz'}, dimensions={0} | all-to-all | bytes 1024 | tf_op jit(solution)/shard_map/all_to_all | solution.py:34
  297.0 16.2 %all_to_all.145 = f32[32,1,4]{2,1,0:T(1,128)S(1)} all-to-all(f32[32,1,4]{2,1,0:T(1,128)S(1)} %broadcast_in_dim.57), channel_id=1, replica_groups=mesh['slab'=2,'py'=16,'pz'=32] {'slab','py'}, dimensions={0} | all-to-all | bytes 1024 | tf_op jit(solution)/shard_map/all_to_all | solution.py:34
  323.8 4.0 collective-permute-start.23
  337.4 13.2 %all_to_all.146 = f32[32,1,4]{2,1,0:T(1,128)S(1)} all-to-all(f32[32,1,4]{2,1,0:T(1,128)S(1)} %broadcast_in_dim.58), channel_id=1, replica_groups=mesh['slab'=2,'py'=16,'pz'=32] {'pz'}, dimensions={0} | all-to-all | bytes 1024 | tf_op jit(solution)/shard_map/all_to_all | solution.py:34
  351.2 5.2 %all-to-all-start.15 = ((f32[32,1,4]{2,1,0:T(1,128)}), f32[32,1,4]{2,1,0:T(1,128)S(1)}, u32[]{:S(2)}, u32[]{:S(2)}) async-start(f32[32,1,4]{2,1,0:T(1,128)} %broadcast_in_dim.59), calls=%async_computation.15 | async-start | bytes 32768 | tf_op jit(solution)/shard_map/all_to_all | solution.py:34
  357.0 11.2 %all-to-all-done.15 = f32[32,1,4]{2,1,0:T(1,128)S(1)} async-done(((f32[32,1,4]{2,1,0:T(1,128)}), f32[32,1,4]{2,1,0:T(1,128)S(1)}, u32[]{:S(2)}, u32[]{:S(2)}) %all-to-all-start.15) | async-done | bytes 544 | tf_op jit(solution)/shard_map/all_to_all | solution.py:34
  378.6 8.0 %all-to-all-done.16 = f32[32,1,5]{2,1,0:T(1,128)S(1)} async-done(((f32[32,1,5]{2,1,0:T(1,128)}), f32[32,1,5]{2,1,0:T(1,128)S(1)}, u32[]{:S(2)}, u32[]{:S(2)}) %all-to-all-start.16) | async-done | bytes 672 | tf_op jit(solution)/shard_map/all_to_all | solution.py:34
  387.2 5.1 %all-to-all-start.17 = ((f32[32,1,5]{2,1,0:T(1,128)}), f32[32,1,5]{2,1,0:T(1,128)S(1)}, u32[]{:S(2)}, u32[]{:S(2)}) async-start(f32[32,1,5]{2,1,0:T(1,128)} %broadcast_in_dim.61), calls=%async_computation.17 | async-start | bytes 32768 | tf_op jit(solution)/shard_map/all_to_all | solution.py:34
  393.6 10.6 %all-to-all-done.17 = f32[32,1,5]{2,1,0:T(1,128)S(1)} async-done(((f32[32,1,5]{2,1,0:T(1,128)}), f32[32,1,5]{2,1,0:T(1,128)S(1)}, u32[]{:S(2)}, u32[]{:S(2)}) %all-to-all-start.17) | async-done | bytes 672 | tf_op jit(solution)/shard_map/all_to_all | solution.py:34
  414.8 4.0 collective-permute-start.29
  428.9 4.7 all-to-all-start.18
  434.8 7.4 %all-to-all-done.18 = f32[32,1,5]{2,1,0:T(1,128)S(1)} async-done(((f32[32,1,5]{2,1,0:T(1,128)}), f32[32,1,5]{2,1,0:T(1,128)S(1)}, u32[]{:S(2)}, u32[]{:S(2)}) %all-to-all-start.18) | async-done | bytes 672 | tf_op jit(solution)/shard_map/all_to_all | solution.py:34
  442.9 5.5 %all-to-all-start.19 = ((f32[32,1,5]{2,1,0:T(1,128)}), f32[32,1,5]{2,1,0:T(1,128)S(1)}, u32[]{:S(2)}, u32[]{:S(2)}) async-start(f32[32,1,5]{2,1,0:T(1,128)} %broadcast_in_dim.63), calls=%async_computation.19 | async-start | bytes 32768 | tf_op jit(solution)/shard_map/all_to_all | solution.py:34
  449.0 11.2 %all-to-all-done.19 = f32[32,1,5]{2,1,0:T(1,128)S(1)} async-done(((f32[32,1,5]{2,1,0:T(1,128)}), f32[32,1,5]{2,1,0:T(1,128)S(1)}, u32[]{:S(2)}, u32[]{:S(2)}) %all-to-all-start.19) | async-done | bytes 672 | tf_op jit(solution)/shard_map/all_to_all | solution.py:34
  471.2 7.3 %all-to-all-done.20 = f32[32,1,6]{2,1,0:T(1,128)S(1)} async-done(((f32[32,1,6]{2,1,0:T(1,128)}), f32[32,1,6]{2,1,0:T(1,128)S(1)}, u32[]{:S(2)}, u32[]{:S(2)}) %all-to-all-start.20) | async-done | bytes 800 | tf_op jit(solution)/shard_map/all_to_all | solution.py:34
  479.2 5.1 %all-to-all-start.21 = ((f32[32,1,6]{2,1,0:T(1,128)}), f32[32,1,6]{2,1,0:T(1,128)S(1)}, u32[]{:S(2)}, u32[]{:S(2)}) async-start(f32[32,1,6]{2,1,0:T(1,128)} %broadcast_in_dim.65), calls=%async_computation.21 | async-start | bytes 32768 | tf_op jit(solution)/shard_map/all_to_all | solution.py:34
  484.9 11.3 %all-to-all-done.21 = f32[32,1,6]{2,1,0:T(1,128)S(1)} async-done(((f32[32,1,6]{2,1,0:T(1,128)}), f32[32,1,6]{2,1,0:T(1,128)S(1)}, u32[]{:S(2)}, u32[]{:S(2)}) %all-to-all-start.21) | async-done | bytes 800 | tf_op jit(solution)/shard_map/all_to_all | solution.py:34
  (203 shorter events, 135.6 us)
Async XLA Ops:
  57.4 14.3 %collective-permute-start.3 = (f32[8,1,128]{2,1,0:T(1,128)S(1)}, f32[8,1,128]{2,1,0:T(1,128)S(1)}, u32[]{:S(2)}, u32[]{:S(2)}) collective-permute-start(f32[8,1,128]{2,1,0:T(1,128)S(1)} %get-tuple-element.49), channel_id=1, source_target_pairs={{32,0},{64,32},{96,64},{128,96},{160,128},{192,160},{224,192},{256... | collective-permute-start | bytes 12296 | tf_op jit(solution)/shard_map/ppermute | solution.py:21
  58.7 14.4 %collective-permute-start = (f32[8,1,128]{2,1,0:T(1,128)S(1)}, f32[8,1,128]{2,1,0:T(1,128)S(1)}, u32[]{:S(2)}, u32[]{:S(2)}) collective-permute-start(f32[8,1,128]{2,1,0:T(1,128)S(1)} %get-tuple-element.50), channel_id=1, source_target_pairs={{0,32},{32,64},{64,96},{96,128},{128,160},{160,192},{192,224},{224... | collective-permute-start | bytes 12296 | tf_op jit(solution)/shard_map/ppermute | solution.py:20
  62.7 12.2 %collective-permute-start.4 = (f32[1,32,128]{2,1,0:T(8,128)S(1)}, f32[1,32,128]{2,1,0:T(8,128)S(1)}, u32[]{:S(2)}, u32[]{:S(2)}) collective-permute-start(f32[1,32,128]{2,1,0:T(8,128)S(1)} %get-tuple-element.47), channel_id=1, source_target_pairs={{1,0},{2,1},{3,2},{4,3},{5,4},{6,5},{7,6},{8,7},{9,8},{10,9},{11,1... | collective-permute-start | bytes 49160 | tf_op jit(solution)/shard_map/ppermute | solution.py:21
  64.0 10.9 %collective-permute-start.5 = (f32[1,32,128]{2,1,0:T(8,128)S(1)}, f32[1,32,128]{2,1,0:T(8,128)S(1)}, u32[]{:S(2)}, u32[]{:S(2)}) collective-permute-start(f32[1,32,128]{2,1,0:T(8,128)S(1)} %get-tuple-element.48), channel_id=1, source_target_pairs={{0,1},{1,2},{2,3},{3,4},{4,5},{5,6},{6,7},{7,8},{8,9},{9,10},{10,1... | collective-permute-start | bytes 49160 | tf_op jit(solution)/shard_map/ppermute | solution.py:20
  68.2 4.9 collective-permute-start.2
  143.2 14.0 %collective-permute-start.9 = (f32[8,1,128]{2,1,0:T(1,128)S(1)}, f32[8,1,128]{2,1,0:T(1,128)S(1)}, u32[]{:S(2)}, u32[]{:S(2)}) collective-permute-start(f32[8,1,128]{2,1,0:T(1,128)S(1)} %get-tuple-element.42), channel_id=1, source_target_pairs={{32,0},{64,32},{96,64},{128,96},{160,128},{192,160},{224,192},{256... | collective-permute-start | bytes 12296 | tf_op jit(solution)/shard_map/ppermute | solution.py:21
  144.5 14.1 %collective-permute-start.6 = (f32[8,1,128]{2,1,0:T(1,128)S(1)}, f32[8,1,128]{2,1,0:T(1,128)S(1)}, u32[]{:S(2)}, u32[]{:S(2)}) collective-permute-start(f32[8,1,128]{2,1,0:T(1,128)S(1)} %get-tuple-element.43), channel_id=1, source_target_pairs={{0,32},{32,64},{64,96},{96,128},{128,160},{160,192},{192,224},{224... | collective-permute-start | bytes 12296 | tf_op jit(solution)/shard_map/ppermute | solution.py:20
  148.5 12.0 %collective-permute-start.10 = (f32[1,32,128]{2,1,0:T(8,128)S(1)}, f32[1,32,128]{2,1,0:T(8,128)S(1)}, u32[]{:S(2)}, u32[]{:S(2)}) collective-permute-start(f32[1,32,128]{2,1,0:T(8,128)S(1)} %get-tuple-element.40), channel_id=1, source_target_pairs={{1,0},{2,1},{3,2},{4,3},{5,4},{6,5},{7,6},{8,7},{9,8},{10,9},{11,1... | collective-permute-start | bytes 49160 | tf_op jit(solution)/shard_map/ppermute | solution.py:21
  149.8 10.7 %collective-permute-start.11 = (f32[1,32,128]{2,1,0:T(8,128)S(1)}, f32[1,32,128]{2,1,0:T(8,128)S(1)}, u32[]{:S(2)}, u32[]{:S(2)}) collective-permute-start(f32[1,32,128]{2,1,0:T(8,128)S(1)} %get-tuple-element.41), channel_id=1, source_target_pairs={{0,1},{1,2},{2,3},{3,4},{4,5},{5,6},{6,7},{7,8},{8,9},{9,10},{10,1... | collective-permute-start | bytes 49160 | tf_op jit(solution)/shard_map/ppermute | solution.py:20
  153.8 4.9 collective-permute-start.8
  230.2 14.0 %collective-permute-start.15 = (f32[8,1,128]{2,1,0:T(1,128)S(1)}, f32[8,1,128]{2,1,0:T(1,128)S(1)}, u32[]{:S(2)}, u32[]{:S(2)}) collective-permute-start(f32[8,1,128]{2,1,0:T(1,128)S(1)} %get-tuple-element.36), channel_id=1, source_target_pairs={{32,0},{64,32},{96,64},{128,96},{160,128},{192,160},{224,192},{256... | collective-permute-start | bytes 12296 | tf_op jit(solution)/shard_map/ppermute | solution.py:21
  231.5 14.2 %collective-permute-start.12 = (f32[8,1,128]{2,1,0:T(1,128)S(1)}, f32[8,1,128]{2,1,0:T(1,128)S(1)}, u32[]{:S(2)}, u32[]{:S(2)}) collective-permute-start(f32[8,1,128]{2,1,0:T(1,128)S(1)} %get-tuple-element.37), channel_id=1, source_target_pairs={{0,32},{32,64},{64,96},{96,128},{128,160},{160,192},{192,224},{224... | collective-permute-start | bytes 12296 | tf_op jit(solution)/shard_map/ppermute | solution.py:20
  235.5 12.0 %collective-permute-start.16 = (f32[1,32,128]{2,1,0:T(8,128)S(1)}, f32[1,32,128]{2,1,0:T(8,128)S(1)}, u32[]{:S(2)}, u32[]{:S(2)}) collective-permute-start(f32[1,32,128]{2,1,0:T(8,128)S(1)} %get-tuple-element.34), channel_id=1, source_target_pairs={{1,0},{2,1},{3,2},{4,3},{5,4},{6,5},{7,6},{8,7},{9,8},{10,9},{11,1... | collective-permute-start | bytes 49160 | tf_op jit(solution)/shard_map/ppermute | solution.py:21
  236.8 10.7 %collective-permute-start.17 = (f32[1,32,128]{2,1,0:T(8,128)S(1)}, f32[1,32,128]{2,1,0:T(8,128)S(1)}, u32[]{:S(2)}, u32[]{:S(2)}) collective-permute-start(f32[1,32,128]{2,1,0:T(8,128)S(1)} %get-tuple-element.35), channel_id=1, source_target_pairs={{0,1},{1,2},{2,3},{3,4},{4,5},{5,6},{6,7},{7,8},{8,9},{9,10},{10,1... | collective-permute-start | bytes 49160 | tf_op jit(solution)/shard_map/ppermute | solution.py:20
  240.8 5.0 collective-permute-start.14
  317.2 14.0 %collective-permute-start.21 = (f32[8,1,128]{2,1,0:T(1,128)S(1)}, f32[8,1,128]{2,1,0:T(1,128)S(1)}, u32[]{:S(2)}, u32[]{:S(2)}) collective-permute-start(f32[8,1,128]{2,1,0:T(1,128)S(1)} %get-tuple-element.30), channel_id=1, source_target_pairs={{32,0},{64,32},{96,64},{128,96},{160,128},{192,160},{224,192},{256... | collective-permute-start | bytes 12296 | tf_op jit(solution)/shard_map/ppermute | solution.py:21
  318.5 14.3 %collective-permute-start.18 = (f32[8,1,128]{2,1,0:T(1,128)S(1)}, f32[8,1,128]{2,1,0:T(1,128)S(1)}, u32[]{:S(2)}, u32[]{:S(2)}) collective-permute-start(f32[8,1,128]{2,1,0:T(1,128)S(1)} %get-tuple-element.31), channel_id=1, source_target_pairs={{0,32},{32,64},{64,96},{96,128},{128,160},{160,192},{192,224},{224... | collective-permute-start | bytes 12296 | tf_op jit(solution)/shard_map/ppermute | solution.py:20
  322.5 12.0 %collective-permute-start.22 = (f32[1,32,128]{2,1,0:T(8,128)S(1)}, f32[1,32,128]{2,1,0:T(8,128)S(1)}, u32[]{:S(2)}, u32[]{:S(2)}) collective-permute-start(f32[1,32,128]{2,1,0:T(8,128)S(1)} %get-tuple-element.28), channel_id=1, source_target_pairs={{1,0},{2,1},{3,2},{4,3},{5,4},{6,5},{7,6},{8,7},{9,8},{10,9},{11,1... | collective-permute-start | bytes 49160 | tf_op jit(solution)/shard_map/ppermute | solution.py:21
  323.8 10.7 %collective-permute-start.23 = (f32[1,32,128]{2,1,0:T(8,128)S(1)}, f32[1,32,128]{2,1,0:T(8,128)S(1)}, u32[]{:S(2)}, u32[]{:S(2)}) collective-permute-start(f32[1,32,128]{2,1,0:T(8,128)S(1)} %get-tuple-element.29), channel_id=1, source_target_pairs={{0,1},{1,2},{2,3},{3,4},{4,5},{5,6},{6,7},{7,8},{8,9},{9,10},{10,1... | collective-permute-start | bytes 49160 | tf_op jit(solution)/shard_map/ppermute | solution.py:20
  327.8 5.1 %collective-permute-start.20 = (f32[8,32,1]{2,1,0:T(8,128)S(1)}, f32[8,32,1]{2,1,0:T(8,128)S(1)}, u32[]{:S(2)}, u32[]{:S(2)}) collective-permute-start(f32[8,32,1]{2,1,0:T(8,128)S(1)} %get-tuple-element.32), channel_id=1, source_target_pairs={{512,0},{513,1},{514,2},{515,3},{516,4},{517,5},{518,6},{519,7},{5... | collective-permute-start | bytes 3080 | tf_op jit(solution)/shard_map/ppermute | solution.py:21
  351.2 17.1 %all-to-all-start.15 = ((f32[32,1,4]{2,1,0:T(1,128)}), f32[32,1,4]{2,1,0:T(1,128)S(1)}, u32[]{:S(2)}, u32[]{:S(2)}) async-start(f32[32,1,4]{2,1,0:T(1,128)} %broadcast_in_dim.59), calls=%async_computation.15 | async-start | bytes 32768 | tf_op jit(solution)/shard_map/all_to_all | solution.py:34
  374.1 12.4 %all-to-all-start.16 = ((f32[32,1,5]{2,1,0:T(1,128)}), f32[32,1,5]{2,1,0:T(1,128)S(1)}, u32[]{:S(2)}, u32[]{:S(2)}) async-start(f32[32,1,5]{2,1,0:T(1,128)} %broadcast_in_dim.60), calls=%async_computation.16 | async-start | bytes 32768 | tf_op jit(solution)/shard_map/all_to_all | solution.py:34
  387.2 17.0 %all-to-all-start.17 = ((f32[32,1,5]{2,1,0:T(1,128)}), f32[32,1,5]{2,1,0:T(1,128)S(1)}, u32[]{:S(2)}, u32[]{:S(2)}) async-start(f32[32,1,5]{2,1,0:T(1,128)} %broadcast_in_dim.61), calls=%async_computation.17 | async-start | bytes 32768 | tf_op jit(solution)/shard_map/all_to_all | solution.py:34
  408.2 14.0 %collective-permute-start.27 = (f32[8,1,128]{2,1,0:T(1,128)S(1)}, f32[8,1,128]{2,1,0:T(1,128)S(1)}, u32[]{:S(2)}, u32[]{:S(2)}) collective-permute-start(f32[8,1,128]{2,1,0:T(1,128)S(1)} %get-tuple-element.24), channel_id=1, source_target_pairs={{32,0},{64,32},{96,64},{128,96},{160,128},{192,160},{224,192},{256... | collective-permute-start | bytes 12296 | tf_op jit(solution)/shard_map/ppermute | solution.py:21
  409.5 14.7 %collective-permute-start.24 = (f32[8,1,128]{2,1,0:T(1,128)S(1)}, f32[8,1,128]{2,1,0:T(1,128)S(1)}, u32[]{:S(2)}, u32[]{:S(2)}) collective-permute-start(f32[8,1,128]{2,1,0:T(1,128)S(1)} %get-tuple-element.25), channel_id=1, source_target_pairs={{0,32},{32,64},{64,96},{96,128},{128,160},{160,192},{192,224},{224... | collective-permute-start | bytes 12296 | tf_op jit(solution)/shard_map/ppermute | solution.py:20
  413.5 12.0 %collective-permute-start.28 = (f32[1,32,128]{2,1,0:T(8,128)S(1)}, f32[1,32,128]{2,1,0:T(8,128)S(1)}, u32[]{:S(2)}, u32[]{:S(2)}) collective-permute-start(f32[1,32,128]{2,1,0:T(8,128)S(1)} %get-tuple-element.22), channel_id=1, source_target_pairs={{1,0},{2,1},{3,2},{4,3},{5,4},{6,5},{7,6},{8,7},{9,8},{10,9},{11,1... | collective-permute-start | bytes 49160 | tf_op jit(solution)/shard_map/ppermute | solution.py:21
  414.8 10.7 %collective-permute-start.29 = (f32[1,32,128]{2,1,0:T(8,128)S(1)}, f32[1,32,128]{2,1,0:T(8,128)S(1)}, u32[]{:S(2)}, u32[]{:S(2)}) collective-permute-start(f32[1,32,128]{2,1,0:T(8,128)S(1)} %get-tuple-element.23), channel_id=1, source_target_pairs={{0,1},{1,2},{2,3},{3,4},{4,5},{5,6},{6,7},{7,8},{8,9},{9,10},{10,1... | collective-permute-start | bytes 49160 | tf_op jit(solution)/shard_map/ppermute | solution.py:20
  418.8 5.5 %collective-permute-start.26 = (f32[8,32,1]{2,1,0:T(8,128)S(1)}, f32[8,32,1]{2,1,0:T(8,128)S(1)}, u32[]{:S(2)}, u32[]{:S(2)}) collective-permute-start(f32[8,32,1]{2,1,0:T(8,128)S(1)} %get-tuple-element.26), channel_id=1, source_target_pairs={{512,0},{513,1},{514,2},{515,3},{516,4},{517,5},{518,6},{519,7},{5... | collective-permute-start | bytes 3080 | tf_op jit(solution)/shard_map/ppermute | solution.py:21
  428.9 13.3 %all-to-all-start.18 = ((f32[32,1,5]{2,1,0:T(1,128)}), f32[32,1,5]{2,1,0:T(1,128)S(1)}, u32[]{:S(2)}, u32[]{:S(2)}) async-start(f32[32,1,5]{2,1,0:T(1,128)} %broadcast_in_dim.62), calls=%async_computation.18 | async-start | bytes 32768 | tf_op jit(solution)/shard_map/all_to_all | solution.py:34
  442.9 17.3 %all-to-all-start.19 = ((f32[32,1,5]{2,1,0:T(1,128)}), f32[32,1,5]{2,1,0:T(1,128)S(1)}, u32[]{:S(2)}, u32[]{:S(2)}) async-start(f32[32,1,5]{2,1,0:T(1,128)} %broadcast_in_dim.63), calls=%async_computation.19 | async-start | bytes 32768 | tf_op jit(solution)/shard_map/all_to_all | solution.py:34
  466.1 12.4 %all-to-all-start.20 = ((f32[32,1,6]{2,1,0:T(1,128)}), f32[32,1,6]{2,1,0:T(1,128)S(1)}, u32[]{:S(2)}, u32[]{:S(2)}) async-start(f32[32,1,6]{2,1,0:T(1,128)} %broadcast_in_dim.64), calls=%async_computation.20 | async-start | bytes 32768 | tf_op jit(solution)/shard_map/all_to_all | solution.py:34
  479.2 17.0 %all-to-all-start.21 = ((f32[32,1,6]{2,1,0:T(1,128)}), f32[32,1,6]{2,1,0:T(1,128)S(1)}, u32[]{:S(2)}, u32[]{:S(2)}) async-start(f32[32,1,6]{2,1,0:T(1,128)} %broadcast_in_dim.65), calls=%async_computation.21 | async-start | bytes 32768 | tf_op jit(solution)/shard_map/all_to_all | solution.py:34
  (8 other events, 84.7 us)
where the time goes:
time: 513 us; the launch traced here: 503 us
  blocking collectives  239 us (47%)
  starting transfers between devices  110 us (21%)
  waiting for transfers between devices  75 us (15%)
  matrix products  29.2 us (6%)
  other arithmetic  19.4 us (4%)
  between operations  16 us (3%)
  local copies, waits for them, and re-layouts  14.8 us (3%)
    all_to_all x15, blocking collectives, sent_to_all(): lax.all_to_all(jnp.broadcast_to(value[None], (peers, *value.shape)), axis...  239 us
    all_to_all x7, waiting for transfers between devices, sent_to_all(): lax.all_to_all(jnp.broadcast_to(value[None], (peers, *value.shape)), axis...  67 us
    ppermute x15, starting transfers between devices, extended(): lax.ppermute(last, axis, up)  46.7 us
    all_to_all x7, starting transfers between devices, sent_to_all(): lax.all_to_all(jnp.broadcast_to(value[None], (peers, *value.shape)), axis...  33.3 us
    ppermute x15, starting transfers between devices, extended(): lax.ppermute(first, axis, [(b, a) for a, b in up])  30 us
    dot_general x8, matrix products, project(): jnp.einsum('kzyx,zyx->k', active, image, precision=lax.Precision.HIGHEST)  19.6 us
  transfers between devices with their start and end apart: 37, of which 12 were waited for; matrix products, arithmetic and copies ran while one was open for 1% of the time, Pallas kernels for 0%

commit v1 on v0

v1 whole, which is shorter than its diff:
```python
import functools

import jax
import jax.numpy as jnp
from jax import lax
from jax.experimental import pallas as pl
from jax.experimental.pallas import tpu as pltpu
from jax.sharding import PartitionSpec as P

ITERS = 5
EPSILON = 1e-06
INTERPRET = False

SHIFTS = (2.25, 14.25, 8.25, 2.25, 14.25)
SCALE = 2.0**40
COUNT = ITERS + 1
PAIRS = [(i, k) for i in range(COUNT) for k in range(i, COUNT)]
EDGE = 8


def two_sum(a, b):
    s = a + b
    t = s - a
    return s, (a - (s - t)) + (b - t)


def split(a):
    c = a * 4097.0
    high = c - (c - a)
    return high, a - high


def pair_add(a, b):
    s, e = two_sum(a[0], b[0])
    e = e + (a[1] + b[1])
    high = s + e
    return high, e - (high - s)


def pair_mul(a, b):
    p = a[0] * b[0]
    ah, al = split(a[0])
    bh, bl = split(b[0])
    e = ((ah * bh - p) + (ah * bl + al * bh)) + al * bl
    e = e + (a[0] * b[1] + a[1] * b[0])
    high = p + e
    return high, e - (high - p)


def pair_neg(a):
    return -a[0], -a[1]


def pair_sum(terms):
    terms = list(terms)
    while len(terms) > 1:
        rest = terms[len(terms) // 2 * 2 :]
        terms = [pair_add(terms[i], terms[i + 1]) for i in range(0, len(terms) - 1, 2)] + rest
    return terms[0]


def over_sublanes(a):
    for shift in (4, 2, 1):
        a = pair_add(a, (pltpu.roll(a[0], shift, 0), pltpu.roll(a[1], shift, 0)))
    return a


def lanes():
    return lax.broadcasted_iota(jnp.int32, (8, 128), 1)


def as_row(a):
    return jnp.where(lanes() < 64, a[0], pltpu.roll(a[1], 64, 1))


def sum_of_rows(ref):
    blocks = [ref[pl.ds(8 * r, 8), :] for r in range(ref.shape[0] // 8)]
    return over_sublanes(pair_sum([(b, pltpu.roll(b, 64, 1)) for b in blocks]))


def assemble(x, k0, dg, slot):
    depth, height = ITERS, 32

    def put(ref, planes, rows, first, factor):
        n, r = planes.stop - planes.start, rows.stop - rows.start
        piece = x[pl.ds(first, n * r), :].reshape(n, r, 128)
        ref[slot, planes, rows, :] = piece * factor
        return first + n * r

    low, own, high = slice(0, 8), slice(8, 40), slice(40, 48)
    at = put(k0, slice(5, 13), own, 0, SCALE)
    at = put(dg, slice(4, 12), own, at, 0.125)
    for rows in (low, high):
        at = put(k0, slice(5, 13), rows, at, SCALE)
        at = put(dg, slice(4, 12), rows, at, 0.125)
    for side in (0, 1):
        at = put(k0, slice(13, 18) if side else slice(0, 5), own, at, SCALE)
        at = put(dg, slice(12, 16) if side else slice(0, 4), own, at, 0.125)
        for rows in (low, high):
            at = put(k0, slice(13, 17) if side else slice(1, 5), rows, at, SCALE)
        for rows in (low, high):
            at = put(dg, slice(12, 15) if side else slice(1, 4), rows, at, 0.125)
    for rows in (low, high):
        for plane in (0, 17):
            k0[slot, plane, rows, :] = jnp.zeros((8, 128), jnp.float32)
        for plane in (0, 15):
            dg[slot, plane, rows, :] = jnp.zeros((8, 128), jnp.float32)


def krylov_kernel(x, q, k_out, row_out, k0, k1, k2, k3, k4, k5, dg):
    mine = lax.axis_index("slab")
    y, z = lax.axis_index("py"), lax.axis_index("pz")
    inside = {
        "y_low": jnp.where(y > 0, 1.0, 0.0),
        "y_high": jnp.where(y < lax.axis_size("py") - 1, 1.0, 0.0),
        "z_low": jnp.where(z > 0, 1.0, 0.0),
        "z_high": jnp.where(z < lax.axis_size("pz") - 1, 1.0, 0.0),
    }
    assemble(x, k0, dg, mine)
    assemble(q, k0, dg, 1 - mine)
    lane = lax.broadcasted_iota(jnp.int32, (48, 128), 1)
    first, last = lane == 0, lane == 127
    basis = (k0, k1, k2, k3, k4, k5)
    for step in range(1, COUNT):
        old, new = basis[step - 1], basis[step]
        shift = (6.0 - SHIFTS[step - 1]) * 0.125
        for plane in range(step, 18 - step):
            f = [old[t, plane] for t in (0, 1)]
            up = [pltpu.roll(a, 1, 1) for a in f]
            down = [pltpu.roll(a, 127, 1) for a in f]
            beside = [
                jnp.where(first, 0.0, up[0]) + jnp.where(last, down[1], down[0]),
                jnp.where(first, up[0], up[1]) + jnp.where(last, 0.0, down[1]),
            ]
            for t in (0, 1):
                around = beside[t] + (pltpu.roll(f[t], 1, 0) + pltpu.roll(f[t], 47, 0))
                around = around + (old[t, plane - 1] + old[t, plane + 1])
                image = (dg[t, plane - 1] + shift) * f[t] - 0.125 * around
                if step == ITERS:
                    new[t, plane - ITERS] = image[8:40]
                    continue
                if plane < ITERS:
                    image = image * inside["z_low"]
                if plane >= 13:
                    image = image * inside["z_high"]
                new[t, plane, 0:8] = image[0:8] * inside["y_low"]
                new[t, plane, 8:40] = image[8:40]
                new[t, plane, 40:48] = image[40:48] * inside["y_high"]
    sums = [None] * len(PAIRS)
    for plane in range(8):
        for tile in range(4):
            own = [b[mine, 5 + plane, 8 + 8 * tile : 16 + 8 * tile] for b in basis[:ITERS]]
            own.append(k5[mine, plane, 8 * tile : 8 + 8 * tile])
            for i, value in enumerate(own):
                k_out[i, plane, 8 * tile : 8 + 8 * tile] = value
            parts = [split(value) for value in own]
            for n, (i, k) in enumerate(PAIRS):
                big = parts[i][0] * parts[k][0]
                small = parts[i][0] * parts[k][1] + parts[i][1] * own[k]
                if sums[n] is None:
                    sums[n] = (big, small)
                else:
                    s, e = two_sum(sums[n][0], big)
                    sums[n] = (s, sums[n][1] + (e + small))
    row = lax.broadcasted_iota(jnp.int32, (8, 128), 0)
    tables = []
    sums = [over_sublanes(s) for s in sums]
    for half in (0, 1):
        blocks = []
        for start in range(0, len(PAIRS), 8):
            block = sums[start][half]
            for n in range(start + 1, min(start + 8, len(PAIRS))):
                block = jnp.where(row == n - start, sums[n][half], block)
            blocks.append(block)
        blocks.append(jnp.zeros((128 - 8 * len(blocks), 128), jnp.float32))
        tables.append(jnp.transpose(jnp.concatenate(blocks)))
    total = over_sublanes(
        pair_sum([tuple(t[8 * r : 8 * r + 8] for t in tables) for r in range(16)])
    )
    sent = as_row(total)
    for r in range(row_out.shape[0] // 8):
        row_out[8 * r : 8 * r + 8] = sent


def rows_kernel(rows, out):
    sent = as_row(sum_of_rows(rows))
    for r in range(out.shape[0] // 8):
        out[8 * r : 8 * r + 8] = sent


def root_of(square):
    x = pair_add(square, (jnp.full_like(square[0], EPSILON), jnp.zeros_like(square[0])))
    r = lax.rsqrt(x[0])
    for _ in range(2):
        r = r * (1.5 - (0.5 * x[0]) * (r * r))
    zero = jnp.zeros_like(r)
    one = pair_mul(x, pair_mul((r, zero), (r, zero)))
    miss = (1.0 - one[0]) - one[1]
    return x[0] * r, (r, r * (0.5 * miss))


def coefficients(gram):
    zero = jnp.zeros((8, 128), jnp.float32)
    _, inverse = root_of(tuple(g * SCALE**-2 for g in gram[0][0]))
    coeffs = [[tuple(r / SCALE for r in inverse)]]
    lack = [[(EPSILON * inverse[0]) * inverse[0]]]
    alphas, betas = [], []
    for j in range(ITERS):
        newest = coeffs[j]
        image = [None] * (j + 2)
        for i in range(j + 2):
            terms = []
            if i <= j:
                terms.append(pair_mul(newest[i], (jnp.full_like(zero, SHIFTS[i]), zero)))
            if i >= 1:
                terms.append((8.0 * newest[i - 1][0], 8.0 * newest[i - 1][1]))
            image[i] = pair_sum(terms)
        weights = [
            pair_sum([pair_mul(gram[i][k], image[k]) for k in range(j + 2)]) for i in range(j + 2)
        ]
        first = [
            pair_sum([pair_mul(coeffs[k][i], weights[i]) for i in range(k + 1)])
            for k in range(j + 1)
        ]
        second = [sum(lack[k][l] * first[l][0] for l in range(j + 1)) for k in range(j + 1)]
        third = [sum(lack[k][l] * second[l] for l in range(j + 1)) for k in range(j + 1)]
        both = [pair_add(first[k], (second[k], zero)) for k in range(j + 1)]
        rest = sum(
            second[k] * second[k] - both[k][0] * (second[k] + third[k]) for k in range(j + 1)
        )
        square = pair_sum(
            [pair_mul(image[i], weights[i]) for i in range(j + 2)]
            + [pair_neg(pair_mul(f, f)) for f in first]
            + [(rest, zero)]
        )
        positive = square[0] + square[1] > 0.0
        beta, inverse = root_of(tuple(jnp.where(positive, s, 0.0) for s in square))
        alphas.append(both[j][0])
        betas.append(beta)
        following = []
        for i in range(j + 2):
            terms = [image[i]] + [
                pair_neg(pair_mul(both[k], coeffs[k][i])) for k in range(i, j + 1)
            ]
            following.append(pair_mul(pair_sum(terms), inverse))
        coeffs.append(following)
        for k in range(j + 1):
            lack[k].append(-third[k] * inverse[0])
        lack.append([lack[k][j + 1] for k in range(j + 1)] + [(EPSILON * inverse[0]) * inverse[0]])
    return coeffs, alphas, betas


def lanczos_kernel(per_cell, rows, basis, vectors, tridiagonal):
    total = sum_of_rows(rows)
    gram = [[None] * COUNT for _ in range(COUNT)]
    for n, (i, k) in enumerate(PAIRS):
        gram[i][k] = gram[k][i] = tuple(
            jnp.broadcast_to(t[:, n : n + 1], (8, 128)) * per_cell for t in total
        )
    coeffs, alphas, betas = coefficients(gram)
    lane = lanes()
    table = [jnp.zeros((8, 128), jnp.float32)] * 2
    for r, values in enumerate((alphas, betas)):
        for j, value in enumerate(values):
            table[r] = jnp.where(lane == j, value, table[r])
        tridiagonal[r : r + 1, :] = table[r][0:1, 0:ITERS]
    final = [[c[0] + c[1] for c in column] for column in coeffs]
    for plane in range(8):
        for tile in range(4):
            rows_of = slice(8 * tile, 8 * tile + 8)
            k = [basis[i, plane, rows_of] for i in range(COUNT)]
            for j, column in enumerate(final):
                value = column[0] * k[0]
                for i in range(1, j + 1):
                    value = value + column[i] * k[i]
                vectors[j, plane, rows_of] = value


def call(kernel, out_shape, scratch=(), flops=10000, mebibytes=4):
    return pl.pallas_call(
        kernel,
        out_shape=out_shape,
        scratch_shapes=list(scratch),
        cost_estimate=pl.CostEstimate(flops=flops, bytes_accessed=flops, transcendentals=0),
        compiler_params=pltpu.CompilerParams(vmem_limit_bytes=mebibytes * 2**20),
        interpret=INTERPRET,
    )


def to_rows(*pieces):
    return jnp.concatenate([p.reshape(-1, 128) for p in pieces])


def shards(v, p):
    f32 = jnp.float32

    def line(axis, step):
        n = lax.axis_size(axis)
        return [(i, i + step) for i in range(n) if 0 <= i + step < n]

    def exchange(to_next, to_previous, axis):
        return (
            lax.ppermute(to_next, axis, line(axis, 1)),
            lax.ppermute(to_previous, axis, line(axis, -1)),
        )

    last, first = slice(32 - EDGE, 32), slice(0, EDGE)
    y_low, y_high = exchange(
        jnp.stack([v[:, last], p[:, last]]), jnp.stack([v[:, first], p[:, first]]), "py"
    )
    z_low, z_high = exchange(
        to_rows(v[3:], p[4:], y_low[0, 4:], y_high[0, 4:], y_low[1, 5:], y_high[1, 5:]),
        to_rows(v[:5], p[:4], y_low[0, :4], y_high[0, :4], y_low[1, :3], y_high[1, :3]),
        "pz",
    )
    x = to_rows(v, p, y_low, y_high, z_low, z_high)
    q = lax.ppermute(x, "slab", [(0, 1), (1, 0)])
    n_z = lax.axis_size("pz")
    n_xy = lax.axis_size("slab") * lax.axis_size("py")
    block = [pltpu.VMEM((2, 18, 48, 128), f32)] * 5
    basis, rows = call(
        krylov_kernel,
        (jax.ShapeDtypeStruct((COUNT, 8, 32, 128), f32), jax.ShapeDtypeStruct((n_z, 128), f32)),
        block + [pltpu.VMEM((2, 8, 32, 128), f32), pltpu.VMEM((2, 16, 48, 128), f32)],
        20000000,
        12,
    )(x, q)
    rows = lax.all_to_all(rows, "pz", 0, 0, tiled=True)
    rows = call(rows_kernel, jax.ShapeDtypeStruct((n_xy, 128), f32))(rows)
    rows = lax.all_to_all(rows, ("slab", "py"), 0, 0, tiled=True)
    per_cell = 1.0 / (v.size * n_z * n_xy)
    return call(
        functools.partial(lanczos_kernel, per_cell),
        (
            jax.ShapeDtypeStruct((COUNT, 8, 32, 128), f32),
            jax.ShapeDtypeStruct((2, ITERS), f32),
        ),
        flops=20000000,
    )(rows, basis)


def solution(mesh):
    in_specs = (P("pz", "py", "slab"), P("pz", "py", "slab"))
    out_specs = (P(None, "pz", "py", "slab"), P())
    return jax.shard_map(shards, mesh=mesh, in_specs=in_specs, out_specs=out_specs, check_vma=False)
```

time: 513 us -> 86.2 us (0.17); the launches traced: 503 us -> 85.9 us
  blocking collectives: 239 us -> 43.4 us
  starting transfers between devices: 110 us -> 25.8 us
  waiting for transfers between devices: 75 us -> 8.74 us
  matrix products: 29.2 us -> 0 us
  other arithmetic: 19.4 us -> 0.01 us
  between operations: 16 us -> 0.84 us
  local copies, waits for them, and re-layouts: 14.8 us -> 0.97 us
  Pallas kernels: 0 us -> 6.16 us
    all_to_all x15 -> x2, blocking collectives: 239 us -> 43.4 us  [the longest x1 31 us: shards(): rows = lax.all_to_all(rows, ('slab', 'py'), 0, 0, tiled=True)]
    all_to_all x7 -> x0, waiting for transfers between devices: 67 us -> none  [sent_to_all(): lax.all_to_all(jnp.broadcast_to(value[None], (peers, *value.shape)), axis...]
    ppermute x30 -> x5, starting transfers between devices: 76.7 us -> 25.8 us  [the longest x1 14.1 us: shards(): q = lax.ppermute(x, 'slab', [(0, 1), (1, 0)])]
    all_to_all x7 -> x0, starting transfers between devices: 33.3 us -> none  [sent_to_all(): lax.all_to_all(jnp.broadcast_to(value[None], (peers, *value.shape)), axis...]
    dot_general x16 -> x0, matrix products: 29.2 us -> none  [the longest x8 19.6 us: project(): jnp.einsum('kzyx,zyx->k', active, image, precision=lax.Precision.HIGHEST)]
    reduce_sum x32 -> x0, other arithmetic: 10.7 us -> none  [the longest x22 3.45 us: of_everyone(): return sent_to_all(value, axis).sum(axis=0)]
    broadcast_in_dim x22 -> x0, local copies, waits for them, and re-layouts: 7.12 us -> none  [sent_to_all(): jnp.broadcast_to(value[None], (peers, *value.shape))]
    pallas_call x0 -> x3, Pallas kernels: none -> 6.16 us  [the longest x1 3.61 us: shards(): call(krylov_kernel, (jax.ShapeDtypeStruct((COUNT, 8, 32, 128), f32), jax....]
  transfers between devices with their start and end apart: 37 -> 5, of which waited for: 12 -> 3; matrix products, arithmetic and copies ran while one was open for 1% -> 0% of each run, Pallas kernels for 0% -> 0%
where the time goes in v1:
time: 86.2 us; the launch traced here: 85.9 us
  blocking collectives  43.4 us (50%)
  starting transfers between devices  25.8 us (30%)
  waiting for transfers between devices  8.74 us (10%)
  Pallas kernels  6.16 us (7%)
  local copies, waits for them, and re-layouts  0.97 us (1%)
    all_to_all x1, blocking collectives, shards(): rows = lax.all_to_all(rows, ('slab', 'py'), 0, 0, tiled=True)  31 us
    ppermute x1, starting transfers between devices, shards(): q = lax.ppermute(x, 'slab', [(0, 1), (1, 0)])  14.1 us
    all_to_all x1, blocking collectives, shards(): rows = lax.all_to_all(rows, 'pz', 0, 0, tiled=True)  12.3 us
    ppermute x2, starting transfers between devices, exchange(): lax.ppermute(to_next, axis, line(axis, 1))  8.95 us
    ppermute x2, waiting for transfers between devices, exchange(): lax.ppermute(to_previous, axis, line(axis, -1))  4.18 us
    pallas_call x1, Pallas kernels, shards(): call(krylov_kernel, (jax.ShapeDtypeStruct((COUNT, 8, 32, 128), f32), jax....  3.61 us
    ppermute x2, starting transfers between devices, exchange(): lax.ppermute(to_previous, axis, line(axis, -1))  2.72 us
    ppermute x2, waiting for transfers between devices, exchange(): lax.ppermute(to_next, axis, line(axis, 1))  2.64 us
  transfers between devices with their start and end apart: 5, of which 3 were waited for; matrix products, arithmetic and copies ran while one was open for 0% of the time, Pallas kernels for 0%

profile of v1, /device:TPU:1, one launch (start us, length us, event | category | flops | bytes accessed | tf_op | source)
XLA Modules:
  0.0 85.9 jit_solution(4049055670180675634)
XLA Ops:
  0.6 0.8 slice_bitcast_fusion
  1.5 0.0 copy-start.1
  1.5 4.9 %collective-permute-start = (f32[2,8,8,128]{3,2,1,0:T(8,128)S(1)}, f32[2,8,8,128]{3,2,1,0:T(8,128)S(1)}, u32[]{:S(2)}, u32[]{:S(2)}) collective-permute-start(f32[2,8,8,128]{3,2,1,0:T(8,128)S(1)} %pad_maximum_fusion), channel_id=1, source_target_pairs={{0,32},{32,64},{64,96},{96,128},{128,160},{160,192},{192,224},{224... | collective-permute-start | bytes 196616 | tf_op jit(solution)/shard_map/ppermute | solution.py:303
  6.5 0.0 copy-start
  6.5 1.4 %collective-permute-start.1 = (f32[2,8,8,128]{3,2,1,0:T(8,128)S(1)}, f32[2,8,8,128]{3,2,1,0:T(8,128)S(1)}, u32[]{:S(2)}, u32[]{:S(2)}) collective-permute-start(f32[2,8,8,128]{3,2,1,0:T(8,128)S(1)} %pad_maximum_fusion.1), channel_id=1, source_target_pairs={{32,0},{64,32},{96,64},{128,96},{160,128},{192,160},{224,192},{256... | collective-permute-start | bytes 196616 | tf_op jit(solution)/shard_map/ppermute | solution.py:304
  7.9 0.0 copy-done.1
  7.9 0.0 copy-done
  8.0 0.0 collective-permute-done
  8.1 4.2 %collective-permute-done.1 = f32[2,8,8,128]{3,2,1,0:T(8,128)S(1)} collective-permute-done((f32[2,8,8,128]{3,2,1,0:T(8,128)S(1)}, f32[2,8,8,128]{3,2,1,0:T(8,128)S(1)}, u32[]{:S(2)}, u32[]{:S(2)}) %collective-permute-start.1) | collective-permute-done | bytes 65568 | tf_op jit(solution)/shard_map/ppermute | solution.py:304
  12.3 1.3 %collective-permute-start.3 = (f32[400,128]{1,0:T(8,128)S(1)}, f32[400,128]{1,0:T(8,128)S(1)}, u32[]{:S(2)}, u32[]{:S(2)}) collective-permute-start(f32[400,128]{1,0:T(8,128)S(1)} %get-tuple-element.14), channel_id=1, source_target_pairs={{1,0},{2,1},{3,2},{4,3},{5,4},{6,5},{7,6},{8,7},{9,8},{10,9},{11,1... | collective-permute-start | bytes 614408 | tf_op jit(solution)/shard_map/ppermute | solution.py:304
  13.6 4.0 %collective-permute-start.2 = (f32[400,128]{1,0:T(8,128)S(1)}, f32[400,128]{1,0:T(8,128)S(1)}, u32[]{:S(2)}, u32[]{:S(2)}) collective-permute-start(f32[400,128]{1,0:T(8,128)S(1)} %get-tuple-element.15), channel_id=1, source_target_pairs={{0,1},{1,2},{2,3},{3,4},{4,5},{5,6},{6,7},{7,8},{8,9},{9,10},{10,1... | collective-permute-start | bytes 614408 | tf_op jit(solution)/shard_map/ppermute | solution.py:303
  17.6 2.6 %collective-permute-done.2 = f32[400,128]{1,0:T(8,128)S(1)} collective-permute-done((f32[400,128]{1,0:T(8,128)S(1)}, f32[400,128]{1,0:T(8,128)S(1)}, u32[]{:S(2)}, u32[]{:S(2)}) %collective-permute-start.2) | collective-permute-done | bytes 204832 | tf_op jit(solution)/shard_map/ppermute | solution.py:303
  20.3 0.0 collective-permute-done.3
  20.3 14.1 %collective-permute-start.4 = (f32[1568,128]{1,0:T(8,128)S(1)}, f32[1568,128]{1,0:T(8,128)S(1)}, u32[]{:S(2)}, u32[]{:S(2)}) collective-permute-start(f32[1568,128]{1,0:T(8,128)S(1)} %constant_dynamic-update-slice_fusion.12.x), channel_id=1, source_target_pairs={{0,512},{512,0},{1,513},{513,1},{2,514},{514,2},{3,515},{515,3},{4... | collective-permute-start | bytes 2408456 | tf_op jit(solution)/shard_map/ppermute | solution.py:317
  34.5 1.9 %collective-permute-done.4.q = f32[1568,128]{1,0:T(8,128)S(1)} collective-permute-done((f32[1568,128]{1,0:T(8,128)S(1)}, f32[1568,128]{1,0:T(8,128)S(1)}, u32[]{:S(2)}, u32[]{:S(2)}) %collective-permute-start.4) | collective-permute-done | bytes 802848 | tf_op jit(solution)/shard_map/ppermute | solution.py:317
  36.4 3.6 %shard_map.41 = (f32[6,8,32,128]{3,2,1,0:T(8,128)S(1)}, f32[32,128]{1,0:T(8,128)S(1)}) custom-call(f32[1568,128]{1,0:T(8,128)S(1)} %constant_dynamic-update-slice_fusion.12.x, f32[1568,128]{1,0:T(8,128)S(1)} %collective-permute-done.4.q), custom_call_target="tpu_custom_call" | custom-call | flops 20000000 | bytes 20000000 | tf_op jit(solution)/shard_map/pallas_call | solution.py:321
  40.0 12.3 %all_to_all.22 = f32[32,1,128]{2,1,0:T(1,128)S(1)} all-to-all(f32[32,1,128]{2,1,0:T(1,128)S(1)} %bitcast.59), channel_id=1, replica_groups=mesh['slab'=2,'py'=16,'pz'=32] {'pz'}, dimensions={0} | all-to-all | bytes 32768 | tf_op jit(solution)/shard_map/all_to_all | solution.py:328
  52.3 0.2 shard_map.42
  52.5 31.0 %all_to_all.23 = f32[32,1,128]{2,1,0:T(1,128)S(1)} all-to-all(f32[32,1,128]{2,1,0:T(1,128)S(1)} %bitcast.58), channel_id=1, replica_groups=mesh['slab'=2,'py'=16,'pz'=32] {'slab','py'}, dimensions={0} | all-to-all | bytes 32768 | tf_op jit(solution)/shard_map/all_to_all | solution.py:330
  83.5 2.4 %shard_map.43 = (f32[6,8,32,128]{3,2,1,0:T(8,128)}, f32[2,5]{1,0:T(2,128)}) custom-call(f32[32,128]{1,0:T(8,128)S(1)} %bitcast.56, f32[6,8,32,128]{3,2,1,0:T(8,128)S(1)} %get-tuple-element.5.basis), custom_call_target="tpu_custom_call" | custom-call | flops 20000000 | bytes 20000000 | tf_op jit(solution)/shard_map/pallas_call | solution.py:332
  (17 shorter events, 0.2 us)
Async XLA Ops:
  1.5 6.4 %copy-start.1 = (f32[8,32,128]{2,1,0:T(8,128)S(1)}, f32[8,32,128]{2,1,0:T(8,128)}, u32[]{:S(2)}) copy-start(f32[8,32,128]{2,1,0:T(8,128)} %param.3) | copy-start | bytes 393220
  1.5 6.6 %collective-permute-start = (f32[2,8,8,128]{3,2,1,0:T(8,128)S(1)}, f32[2,8,8,128]{3,2,1,0:T(8,128)S(1)}, u32[]{:S(2)}, u32[]{:S(2)}) collective-permute-start(f32[2,8,8,128]{3,2,1,0:T(8,128)S(1)} %pad_maximum_fusion), channel_id=1, source_target_pairs={{0,32},{32,64},{64,96},{96,128},{128,160},{160,192},{192,224},{224... | collective-permute-start | bytes 196616 | tf_op jit(solution)/shard_map/ppermute | solution.py:303
  6.5 1.5 %copy-start = (f32[8,32,128]{2,1,0:T(8,128)S(1)}, f32[8,32,128]{2,1,0:T(8,128)}, u32[]{:S(2)}) copy-start(f32[8,32,128]{2,1,0:T(8,128)} %param.2) | copy-start | bytes 393220
  6.5 5.8 %collective-permute-start.1 = (f32[2,8,8,128]{3,2,1,0:T(8,128)S(1)}, f32[2,8,8,128]{3,2,1,0:T(8,128)S(1)}, u32[]{:S(2)}, u32[]{:S(2)}) collective-permute-start(f32[2,8,8,128]{3,2,1,0:T(8,128)S(1)} %pad_maximum_fusion.1), channel_id=1, source_target_pairs={{32,0},{64,32},{96,64},{128,96},{160,128},{192,160},{224,192},{256... | collective-permute-start | bytes 196616 | tf_op jit(solution)/shard_map/ppermute | solution.py:304
  12.3 8.0 %collective-permute-start.3 = (f32[400,128]{1,0:T(8,128)S(1)}, f32[400,128]{1,0:T(8,128)S(1)}, u32[]{:S(2)}, u32[]{:S(2)}) collective-permute-start(f32[400,128]{1,0:T(8,128)S(1)} %get-tuple-element.14), channel_id=1, source_target_pairs={{1,0},{2,1},{3,2},{4,3},{5,4},{6,5},{7,6},{8,7},{9,8},{10,9},{11,1... | collective-permute-start | bytes 614408 | tf_op jit(solution)/shard_map/ppermute | solution.py:304
  13.6 6.7 %collective-permute-start.2 = (f32[400,128]{1,0:T(8,128)S(1)}, f32[400,128]{1,0:T(8,128)S(1)}, u32[]{:S(2)}, u32[]{:S(2)}) collective-permute-start(f32[400,128]{1,0:T(8,128)S(1)} %get-tuple-element.15), channel_id=1, source_target_pairs={{0,1},{1,2},{2,3},{3,4},{4,5},{5,6},{6,7},{7,8},{8,9},{9,10},{10,1... | collective-permute-start | bytes 614408 | tf_op jit(solution)/shard_map/ppermute | solution.py:303
  20.3 16.1 %collective-permute-start.4 = (f32[1568,128]{1,0:T(8,128)S(1)}, f32[1568,128]{1,0:T(8,128)S(1)}, u32[]{:S(2)}, u32[]{:S(2)}) collective-permute-start(f32[1568,128]{1,0:T(8,128)S(1)} %constant_dynamic-update-slice_fusion.12.x), channel_id=1, source_target_pairs={{0,512},{512,0},{1,513},{513,1},{2,514},{514,2},{3,515},{515,3},{4... | collective-permute-start | bytes 2408456 | tf_op jit(solution)/shard_map/ppermute | solution.py:317

commit v2 on v1

v2 whole, which is shorter than its diff:
```python
import functools

import jax
import jax.numpy as jnp
from jax import lax
from jax.experimental import pallas as pl
from jax.experimental.pallas import tpu as pltpu
from jax.sharding import PartitionSpec as P

ITERS = 5
EPSILON = 1e-06
INTERPRET = False

SHIFTS = (2.25, 14.25, 8.25, 2.25, 14.25)
SCALE = 2.0**24
FIRST = 6.0 - SHIFTS[0]
COUNT = ITERS + 1
PAIRS = [(i, k) for i in range(COUNT) for k in range(i, COUNT)]


def two_sum(a, b):
    s = a + b
    t = s - a
    return s, (a - (s - t)) + (b - t)


def split(a):
    c = a * 4097.0
    high = c - (c - a)
    return high, a - high


def pair_add(a, b):
    s, e = two_sum(a[0], b[0])
    e = e + (a[1] + b[1])
    high = s + e
    return high, e - (high - s)


def pair_mul(a, b):
    p = a[0] * b[0]
    ah, al = split(a[0])
    bh, bl = split(b[0])
    e = ((ah * bh - p) + (ah * bl + al * bh)) + al * bl
    return p, e + (a[0] * b[1] + a[1] * b[0])


def pair_times(a, b):
    p = a[0] * b
    ah, al = split(a[0])
    bh, bl = split(b)
    e = ((ah * bh - p) + (ah * bl + al * bh)) + al * bl
    return p, e + a[1] * b


def pair_neg(a):
    return -a[0], -a[1]


def pair_sum(terms):
    terms = list(terms)
    while len(terms) > 1:
        rest = terms[len(terms) // 2 * 2 :]
        terms = [pair_add(terms[i], terms[i + 1]) for i in range(0, len(terms) - 1, 2)] + rest
    return terms[0]


def over_sublanes(a):
    for shift in (4, 2, 1):
        a = pair_add(a, (pltpu.roll(a[0], shift, 0), pltpu.roll(a[1], shift, 0)))
    return a


def lanes():
    return lax.broadcasted_iota(jnp.int32, (8, 128), 1)


def as_row(a):
    return jnp.where(lanes() < 64, a[0], pltpu.roll(a[1], 64, 1))


def sum_of_rows(ref):
    blocks = [ref[pl.ds(8 * r, 8), :] for r in range(ref.shape[0] // 8)]
    return over_sublanes(pair_sum([(b, pltpu.roll(b, 64, 1)) for b in blocks]))


def edges_kernel(v_last, v_first, p_last, p_first, to_next, to_previous):
    to_next[0:8, 0:3] = p_last[:, 5:8]
    to_next[0:8, 3:8] = v_last[:, 3:8]
    to_previous[0:8, 0:5] = v_first[:, 0:5]
    to_previous[0:8, 5:8] = p_first[:, 0:3]
    for plane in range(8):
        to_next[8, plane : plane + 1] = p_last[plane, 4:5]
        to_previous[8, plane : plane + 1] = p_first[plane, 3:4]


def assemble(x, k0, dg, slot):
    def rows_of(at, n):
        return x[pl.ds(at, n), :]

    k0[slot, 5:13, 8:40] = rows_of(0, 256).reshape(8, 32, 128) * SCALE
    dg[slot, 4:12, 8:40] = rows_of(256, 256).reshape(8, 32, 128) + FIRST
    row = lax.broadcasted_iota(jnp.int32, (8, 128), 0)

    def halo(at, high, plane, fourth=None):
        tile = rows_of(at, 8)
        rows = slice(40, 48) if high else slice(0, 8)
        k0[slot, plane, rows] = tile * SCALE
        near = pltpu.roll(tile, 3 if high else 5, 0)
        if fourth is not None:
            far = jnp.broadcast_to(x[pl.ds(fourth, 1), :], (8, 128))
            near = jnp.where(row == (3 if high else 4), far, near)
        dg[slot, plane - 1, rows] = near + FIRST

    for high in (0, 1):
        start = 512 + 72 * high
        for plane in range(8):
            halo(start + 8 * plane, high, 5 + plane, start + 64 + plane)
    for side in (0, 1):
        start = 656 + 352 * side
        own, at = (13, 12) if side else (0, 0)
        k0[slot, own : own + 5, 8:40] = rows_of(start, 160).reshape(5, 32, 128) * SCALE
        dg[slot, at : at + 4, 8:40] = rows_of(start + 160, 128).reshape(4, 32, 128) + FIRST
        for high in (0, 1):
            for plane in range(4):
                halo(start + 288 + 32 * high + 8 * plane, high, (13 if side else 1) + plane)


def krylov_kernel(x, q, k_out, row_out, k0, k1, k2, k3, k4, k5, dg):
    mine = lax.axis_index("slab")
    y, z = lax.axis_index("py"), lax.axis_index("pz")
    inside = {
        "y_low": jnp.where(y > 0, 1.0, 0.0),
        "y_high": jnp.where(y < lax.axis_size("py") - 1, 1.0, 0.0),
        "z_low": jnp.where(z > 0, 1.0, 0.0),
        "z_high": jnp.where(z < lax.axis_size("pz") - 1, 1.0, 0.0),
    }
    assemble(x, k0, dg, mine)
    assemble(q, k0, dg, 1 - mine)
    lane = lax.broadcasted_iota(jnp.int32, (48, 128), 1)
    first, last = lane == 0, lane == 127
    basis = (k0, k1, k2, k3, k4, k5)
    for step in range(1, COUNT):
        old, new = basis[step - 1], basis[step]
        shift = SHIFTS[0] - SHIFTS[step - 1]
        for plane in range(step, 18 - step):
            f = [old[t, plane] for t in (0, 1)]
            up = [pltpu.roll(a, 1, 1) for a in f]
            down = [pltpu.roll(a, 127, 1) for a in f]
            beside = [
                jnp.where(first, 0.0, up[0]) + jnp.where(last, down[1], down[0]),
                jnp.where(first, up[0], up[1]) + jnp.where(last, 0.0, down[1]),
            ]
            outer = step == ITERS or plane in (step, 17 - step)
            rows = slice(8, 40) if outer else slice(0, 48)
            for t in (0, 1):
                along_y = old[t, plane, 7:39] + old[t, plane, 9:41]
                if not outer:
                    along_y = jnp.concatenate(
                        [
                            pltpu.roll(f[t][0:8], 1, 0) + old[t, plane, 1:9],
                            along_y,
                            old[t, plane, 39:47] + pltpu.roll(f[t][40:48], 7, 0),
                        ]
                    )
                around = beside[t][rows] + along_y
                around = around + (old[t, plane - 1, rows] + old[t, plane + 1, rows])
                factor = dg[t, plane - 1, rows]
                if shift != 0.0:
                    factor = factor + shift
                image = factor * f[t][rows] - around
                if step == ITERS:
                    new[t, plane - ITERS] = image
                    continue
                if plane < ITERS:
                    image = image * inside["z_low"]
                if plane >= 13:
                    image = image * inside["z_high"]
                if outer:
                    new[t, plane, rows] = image
                    continue
                new[t, plane, 0:8] = image[0:8] * inside["y_low"]
                new[t, plane, 8:40] = image[8:40]
                new[t, plane, 40:48] = image[40:48] * inside["y_high"]
    sums = [None] * len(PAIRS)
    for plane in range(8):
        for tile in range(4):
            own = [b[mine, 5 + plane, 8 + 8 * tile : 16 + 8 * tile] for b in basis[:ITERS]]
            own.append(k5[mine, plane, 8 * tile : 8 + 8 * tile])
            for i, value in enumerate(own):
                k_out[i, plane, 8 * tile : 8 + 8 * tile] = value
            parts = [split(value) for value in own]
            for n, (i, k) in enumerate(PAIRS):
                big = parts[i][0] * parts[k][0]
                small = parts[i][0] * parts[k][1] + parts[i][1] * own[k]
                if sums[n] is None:
                    sums[n] = (big, small)
                else:
                    s, e = two_sum(sums[n][0], big)
                    sums[n] = (s, sums[n][1] + (e + small))
    row = lax.broadcasted_iota(jnp.int32, (8, 128), 0)
    tables = []
    sums = [over_sublanes(s) for s in sums]
    for half in (0, 1):
        blocks = []
        for start in range(0, len(PAIRS), 8):
            block = sums[start][half]
            for n in range(start + 1, min(start + 8, len(PAIRS))):
                block = jnp.where(row == n - start, sums[n][half], block)
            blocks.append(block)
        blocks.append(jnp.zeros((128 - 8 * len(blocks), 128), jnp.float32))
        tables.append(jnp.transpose(jnp.concatenate(blocks)))
    total = over_sublanes(
        pair_sum([tuple(t[8 * r : 8 * r + 8] for t in tables) for r in range(16)])
    )
    sent = as_row(total)
    for r in range(row_out.shape[0] // 8):
        row_out[8 * r : 8 * r + 8] = sent


def rows_kernel(rows, out):
    sent = as_row(sum_of_rows(rows))
    for r in range(out.shape[0] // 8):
        out[8 * r : 8 * r + 8] = sent


def root_of(square):
    x = pair_add(square, (jnp.full_like(square[0], EPSILON), jnp.zeros_like(square[0])))
    r = lax.rsqrt(x[0])
    r = r * (1.5 - (0.5 * x[0]) * (r * r))
    one = pair_times(pair_times(x, r), r)
    miss = (1.0 - one[0]) - one[1]
    return x[0] * r, (r, r * (0.5 * miss))


def row_of(a, i):
    return tuple(jnp.broadcast_to(t[i : i + 1, :], (8, 128)) for t in a)


def pair_dot(a, b):
    return over_sublanes(pair_mul(a, b))


def coefficients(gram, ready):
    row = lax.broadcasted_iota(jnp.int32, (8, 128), 0)
    zero = jnp.zeros((8, 128), jnp.float32)
    shifts = zero
    for i, shift in enumerate(SHIFTS):
        shifts = jnp.where(row == i, shift, shifts)
    _, inverse = root_of(tuple(g * SCALE**-2 for g in row_of(gram[0], 0)))
    columns = [(jnp.where(row == 0, 1.0, zero), zero)]
    sizes = [tuple(r / SCALE for r in inverse)]
    lack = [[(EPSILON * inverse[0]) * inverse[0]]]
    alphas, betas = [], []
    for j in range(ITERS):
        newest = columns[j]
        image = pair_add(
            pair_times(newest, shifts), tuple(pltpu.roll(t, 1, 0) for t in newest)
        )
        weights = pair_sum([pair_mul(gram[k], row_of(image, k)) for k in range(j + 2)])
        dots = [pair_dot(columns[k], weights) for k in range(j + 1)]
        norm = pair_dot(image, weights)
        ready(j, columns[j], sizes[j])
        first = [pair_mul(dots[k], sizes[k]) for k in range(j + 1)]
        second = [sum(lack[k][l] * first[l][0] for l in range(j + 1)) for k in range(j + 1)]
        third = [sum(lack[k][l] * second[l] for l in range(j + 1)) for k in range(j + 1)]
        both = [pair_add(first[k], (second[k], zero)) for k in range(j + 1)]
        rest = sum(
            second[k] * second[k] - both[k][0] * (second[k] + third[k]) for k in range(j + 1)
        )
        square = pair_sum(
            [norm] + [pair_neg(pair_mul(f, f)) for f in first] + [(rest, zero)]
        )
        square = pair_mul(square, pair_mul(sizes[j], sizes[j]))
        positive = square[0] + square[1] > 0.0
        beta, inverse = root_of(tuple(jnp.where(positive, s, 0.0) for s in square))
        alphas.append(both[j][0] * sizes[j][0])
        betas.append(beta)
        columns.append(
            pair_sum(
                [image]
                + [
                    pair_neg(pair_mul(columns[k], pair_mul(both[k], sizes[k])))
                    for k in range(j + 1)
                ]
            )
        )
        sizes.append(pair_mul(sizes[j], inverse))
        for k in range(j + 1):
            lack[k].append(-third[k] * sizes[j + 1][0])
        lack.append([lack[k][j + 1] for k in range(j + 1)] + [(EPSILON * inverse[0]) * inverse[0]])
    ready(ITERS, columns[ITERS], sizes[ITERS])
    return alphas, betas


def lanczos_kernel(per_cell, rows, basis, vectors, tridiagonal, made, done):
    total = sum_of_rows(rows)
    lane, row = lanes(), lax.broadcasted_iota(jnp.int32, (8, 128), 0)
    gram = []
    for k in range(COUNT):
        low, high = jnp.minimum(row, k), jnp.maximum(row, k)
        place = low * COUNT - ((low * (low - 1)) >> 1) + (high - low)
        picked = (lane == place) & (row < COUNT)
        gram.append(
            tuple(
                jnp.broadcast_to(
                    jnp.sum(jnp.where(picked, t, 0.0), axis=1, keepdims=True) * per_cell, (8, 128)
                )
                for t in total
            )
        )

    def copy(j):
        return pltpu.make_async_copy(made.at[j], vectors.at[j], done.at[j])

    def ready(j, column, size):
        scaled = pair_mul(column, size)
        scaled = scaled[0] + scaled[1]
        factors = [jnp.broadcast_to(scaled[i : i + 1, :], (8, 128)) for i in range(j + 1)]
        for plane in range(8):
            for tile in range(4):
                at = slice(8 * tile, 8 * tile + 8)
                value = factors[0] * basis[0, plane, at]
                for i in range(1, j + 1):
                    value = value + factors[i] * basis[i, plane, at]
                made[j, plane, at] = value
        copy(j).start()

    alphas, betas = coefficients(gram, ready)
    for r, values in enumerate((alphas, betas)):
        table = jnp.zeros((8, 128), jnp.float32)
        for j, value in enumerate(values):
            table = jnp.where(lane == j, value, table)
        tridiagonal[r : r + 1, :] = table[0:1, 0:ITERS]
    for j in range(COUNT):
        copy(j).wait()


def call(kernel, out_shape, scratch=(), flops=10000, mebibytes=4, **specs):
    return pl.pallas_call(
        kernel,
        out_shape=out_shape,
        scratch_shapes=list(scratch),
        cost_estimate=pl.CostEstimate(flops=flops, bytes_accessed=flops, transcendentals=0),
        compiler_params=pltpu.CompilerParams(
            vmem_limit_bytes=mebibytes and mebibytes * 2**20
        ),
        interpret=INTERPRET,
        **specs,
    )


def to_rows(*pieces):
    return jnp.concatenate([p.reshape(-1, 128) for p in pieces])


def shards(v, p):
    f32 = jnp.float32

    def line(axis, step):
        n = lax.axis_size(axis)
        return [(i, i + step) for i in range(n) if 0 <= i + step < n]

    def exchange(to_next, to_previous, axis):
        return (
            lax.ppermute(to_next, axis, line(axis, 1)),
            lax.ppermute(to_previous, axis, line(axis, -1)),
        )

    halo = jax.ShapeDtypeStruct((9, 8, 128), f32)
    last, first = slice(24, 32), slice(0, 8)
    y_low, y_high = exchange(
        *call(edges_kernel, (halo, halo), mebibytes=1)(
            v[:, last], v[:, first], p[:, last], p[:, first]
        ),
        "py",
    )
    z_low, z_high = exchange(
        to_rows(v[3:], p[4:], y_low[4:8], y_high[4:8]),
        to_rows(v[:5], p[:4], y_low[:4], y_high[:4]),
        "pz",
    )
    x = to_rows(v, p, y_low, y_high, z_low, z_high)
    q = lax.ppermute(x, "slab", [(0, 1), (1, 0)])
    n_z = lax.axis_size("pz")
    n_xy = lax.axis_size("slab") * lax.axis_size("py")
    block = [pltpu.VMEM((2, 18, 48, 128), f32)] * 5
    basis, rows = call(
        krylov_kernel,
        (jax.ShapeDtypeStruct((COUNT, 8, 32, 128), f32), jax.ShapeDtypeStruct((n_z, 128), f32)),
        block + [pltpu.VMEM((2, 8, 32, 128), f32), pltpu.VMEM((2, 16, 48, 128), f32)],
        20000000,
        12,
    )(x, q)
    rows = lax.all_to_all(rows, "pz", 0, 0, tiled=True)
    rows = call(rows_kernel, jax.ShapeDtypeStruct((n_xy, 128), f32))(rows)
    rows = lax.all_to_all(rows, ("slab", "py"), 0, 0, tiled=True)
    per_cell = 1.0 / (v.size * n_z * n_xy)
    return call(
        functools.partial(lanczos_kernel, per_cell),
        (
            jax.ShapeDtypeStruct((COUNT, 8, 32, 128), f32),
            jax.ShapeDtypeStruct((2, ITERS), f32),
        ),
        [pltpu.VMEM((COUNT, 8, 32, 128), f32), pltpu.SemaphoreType.DMA((COUNT,))],
        flops=20000000,
        out_specs=(
            pl.BlockSpec(memory_space=pl.ANY),
            pl.BlockSpec(memory_space=pltpu.VMEM),
        ),
    )(rows, basis)


def solution(mesh):
    in_specs = (P("pz", "py", "slab"), P("pz", "py", "slab"))
    out_specs = (P(None, "pz", "py", "slab"), P())
    return jax.shard_map(shards, mesh=mesh, in_specs=in_specs, out_specs=out_specs, check_vma=False)
```

time: 86.2 us -> 85.1 us (0.987)
  starting transfers between devices: 25.8 us -> 23.1 us
  waiting for transfers between devices: 8.74 us -> 10.6 us
    ppermute x2, waiting for transfers between devices: 4.18 us -> 7.76 us  [exchange(): lax.ppermute(to_previous, axis, line(axis, -1))]
    ppermute x1, starting transfers between devices: 14.1 us -> 12.2 us  [shards(): q = lax.ppermute(x, 'slab', [(0, 1), (1, 0)])]
    ppermute x2, waiting for transfers between devices: 2.64 us -> 1.06 us  [exchange(): lax.ppermute(to_next, axis, line(axis, 1))]
    all_to_all x1, blocking collectives: 31 us -> 32 us  [shards(): rows = lax.all_to_all(rows, ('slab', 'py'), 0, 0, tiled=True)]
  transfers between devices with their start and end apart: 5 -> 5, of which waited for: 3 -> 4; matrix products, arithmetic and copies ran while one was open for 0% -> 0% of each run, Pallas kernels for 0% -> 0%
where the time goes in v2:
time: 85.1 us; the launch traced here: 84.8 us
  blocking collectives  43.7 us (51%)
  starting transfers between devices  23.1 us (27%)
  waiting for transfers between devices  10.6 us (12%)
  Pallas kernels  5.64 us (7%)
  local copies, waits for them, and re-layouts  0.93 us (1%)
    all_to_all x1, blocking collectives, shards(): rows = lax.all_to_all(rows, ('slab', 'py'), 0, 0, tiled=True)  32 us
    ppermute x1, starting transfers between devices, shards(): q = lax.ppermute(x, 'slab', [(0, 1), (1, 0)])  12.2 us
    all_to_all x1, blocking collectives, shards(): rows = lax.all_to_all(rows, 'pz', 0, 0, tiled=True)  11.6 us
    ppermute x2, starting transfers between devices, exchange(): lax.ppermute(to_next, axis, line(axis, 1))  8.16 us
    ppermute x2, waiting for transfers between devices, exchange(): lax.ppermute(to_previous, axis, line(axis, -1))  7.76 us
    pallas_call x1, Pallas kernels, shards(): call(krylov_kernel, (jax.ShapeDtypeStruct((COUNT, 8, 32, 128), f32), jax....  3.17 us
    ppermute x2, starting transfers between devices, exchange(): lax.ppermute(to_previous, axis, line(axis, -1))  2.72 us
    pallas_call x1, Pallas kernels, shards(): call(functools.partial(lanczos_kernel, per_cell), (jax.ShapeDtypeStruct((...  2.28 us
  transfers between devices with their start and end apart: 5, of which 4 were waited for; matrix products, arithmetic and copies ran while one was open for 0% of the time, Pallas kernels for 0%

profile of v2, /device:TPU:1, one launch (start us, length us, event | category | flops | bytes accessed | tf_op | source)
XLA Modules:
  0.0 84.8 jit_solution(1651779087076354855)
XLA Ops:
  0.6 0.8 fusion.2
  1.5 0.0 copy-start.1
  1.5 4.9 %collective-permute-start = (f32[9,8,128]{2,1,0:T(8,128)S(1)}, f32[9,8,128]{2,1,0:T(8,128)S(1)}, u32[]{:S(2)}, u32[]{:S(2)}) collective-permute-start(f32[9,8,128]{2,1,0:T(8,128)S(1)} %get-tuple-element.6), channel_id=1, source_target_pairs={{0,32},{32,64},{64,96},{96,128},{128,160},{160,192},{192,224},{224... | collective-permute-start | bytes 110600 | tf_op jit(solution)/shard_map/ppermute | solution.py:366
  6.5 0.0 copy-start
  6.5 1.4 %collective-permute-start.1 = (f32[9,8,128]{2,1,0:T(8,128)S(1)}, f32[9,8,128]{2,1,0:T(8,128)S(1)}, u32[]{:S(2)}, u32[]{:S(2)}) collective-permute-start(f32[9,8,128]{2,1,0:T(8,128)S(1)} %get-tuple-element.7), channel_id=1, source_target_pairs={{32,0},{64,32},{96,64},{128,96},{160,128},{192,160},{224,192},{256... | collective-permute-start | bytes 110600 | tf_op jit(solution)/shard_map/ppermute | solution.py:367
  7.9 0.0 copy-done.1
  7.9 0.0 copy-done
  8.0 0.0 collective-permute-done
  8.0 3.9 %collective-permute-done.1 = f32[9,8,128]{2,1,0:T(8,128)S(1)} collective-permute-done((f32[9,8,128]{2,1,0:T(8,128)S(1)}, f32[9,8,128]{2,1,0:T(8,128)S(1)}, u32[]{:S(2)}, u32[]{:S(2)}) %collective-permute-start.1) | collective-permute-done | bytes 36896 | tf_op jit(solution)/shard_map/ppermute | solution.py:367
  12.0 3.2 %collective-permute-start.2 = (f32[352,128]{1,0:T(8,128)S(1)}, f32[352,128]{1,0:T(8,128)S(1)}, u32[]{:S(2)}, u32[]{:S(2)}) collective-permute-start(f32[352,128]{1,0:T(8,128)S(1)} %pad_maximum_fusion), channel_id=1, source_target_pairs={{0,1},{1,2},{2,3},{3,4},{4,5},{5,6},{6,7},{7,8},{8,9},{9,10},{10,1... | collective-permute-start | bytes 540680 | tf_op jit(solution)/shard_map/ppermute | solution.py:366
  15.2 1.3 %collective-permute-start.3 = (f32[352,128]{1,0:T(8,128)S(1)}, f32[352,128]{1,0:T(8,128)S(1)}, u32[]{:S(2)}, u32[]{:S(2)}) collective-permute-start(f32[352,128]{1,0:T(8,128)S(1)} %pad_maximum_fusion.1), channel_id=1, source_target_pairs={{1,0},{2,1},{3,2},{4,3},{5,4},{6,5},{7,6},{8,7},{9,8},{10,9},{11,1... | collective-permute-start | bytes 540680 | tf_op jit(solution)/shard_map/ppermute | solution.py:367
  16.5 1.1 %collective-permute-done.2 = f32[352,128]{1,0:T(8,128)S(1)} collective-permute-done((f32[352,128]{1,0:T(8,128)S(1)}, f32[352,128]{1,0:T(8,128)S(1)}, u32[]{:S(2)}, u32[]{:S(2)}) %collective-permute-start.2) | collective-permute-done | bytes 180256 | tf_op jit(solution)/shard_map/ppermute | solution.py:366
  17.6 3.8 %collective-permute-done.3 = f32[352,128]{1,0:T(8,128)S(1)} collective-permute-done((f32[352,128]{1,0:T(8,128)S(1)}, f32[352,128]{1,0:T(8,128)S(1)}, u32[]{:S(2)}, u32[]{:S(2)}) %collective-permute-start.3) | collective-permute-done | bytes 180256 | tf_op jit(solution)/shard_map/ppermute | solution.py:367
  21.5 12.2 %collective-permute-start.4 = (f32[1360,128]{1,0:T(8,128)S(1)}, f32[1360,128]{1,0:T(8,128)S(1)}, u32[]{:S(2)}, u32[]{:S(2)}) collective-permute-start(f32[1360,128]{1,0:T(8,128)S(1)} %constant_dynamic-update-slice_fusion.x), channel_id=1, source_target_pairs={{0,512},{512,0},{1,513},{513,1},{2,514},{514,2},{3,515},{515,3},{4... | collective-permute-start | bytes 2088968 | tf_op jit(solution)/shard_map/ppermute | solution.py:384
  33.7 1.8 %collective-permute-done.4.q = f32[1360,128]{1,0:T(8,128)S(1)} collective-permute-done((f32[1360,128]{1,0:T(8,128)S(1)}, f32[1360,128]{1,0:T(8,128)S(1)}, u32[]{:S(2)}, u32[]{:S(2)}) %collective-permute-start.4) | collective-permute-done | bytes 696352 | tf_op jit(solution)/shard_map/ppermute | solution.py:384
  35.5 3.2 %shard_map.42 = (f32[6,8,32,128]{3,2,1,0:T(8,128)S(1)}, f32[32,128]{1,0:T(8,128)S(1)}) custom-call(f32[1360,128]{1,0:T(8,128)S(1)} %constant_dynamic-update-slice_fusion.x, f32[1360,128]{1,0:T(8,128)S(1)} %collective-permute-done.4.q), custom_call_target="tpu_custom_call" | custom-call | flops 20000000 | bytes 20000000 | tf_op jit(solution)/shard_map/pallas_call | solution.py:388
  38.6 11.6 %all_to_all.22 = f32[32,1,128]{2,1,0:T(1,128)S(1)} all-to-all(f32[32,1,128]{2,1,0:T(1,128)S(1)} %bitcast.29), channel_id=1, replica_groups=mesh['slab'=2,'py'=16,'pz'=32] {'pz'}, dimensions={0} | all-to-all | bytes 32768 | tf_op jit(solution)/shard_map/all_to_all | solution.py:395
  50.3 0.2 shard_map.43
  50.4 32.0 %all_to_all.23 = f32[32,1,128]{2,1,0:T(1,128)S(1)} all-to-all(f32[32,1,128]{2,1,0:T(1,128)S(1)} %bitcast.28), channel_id=1, replica_groups=mesh['slab'=2,'py'=16,'pz'=32] {'slab','py'}, dimensions={0} | all-to-all | bytes 32768 | tf_op jit(solution)/shard_map/all_to_all | solution.py:397
  82.5 2.3 %shard_map.44 = (f32[6,8,32,128]{3,2,1,0:T(8,128)}, f32[2,5]{1,0:T(2,128)}) custom-call(f32[32,128]{1,0:T(8,128)S(1)} %bitcast.26, f32[6,8,32,128]{3,2,1,0:T(8,128)S(1)} %get-tuple-element.9.basis), custom_call_target="tpu_custom_call" | custom-call | flops 20000000 | bytes 20000000 | tf_op jit(solution)/shard_map/pallas_call | solution.py:399
  (13 shorter events, 0.1 us)
Async XLA Ops:
  1.5 6.4 %copy-start.1 = (f32[8,32,128]{2,1,0:T(8,128)S(1)}, f32[8,32,128]{2,1,0:T(8,128)}, u32[]{:S(2)}) copy-start(f32[8,32,128]{2,1,0:T(8,128)} %param.3) | copy-start | bytes 393220
  1.5 6.5 %collective-permute-start = (f32[9,8,128]{2,1,0:T(8,128)S(1)}, f32[9,8,128]{2,1,0:T(8,128)S(1)}, u32[]{:S(2)}, u32[]{:S(2)}) collective-permute-start(f32[9,8,128]{2,1,0:T(8,128)S(1)} %get-tuple-element.6), channel_id=1, source_target_pairs={{0,32},{32,64},{64,96},{96,128},{128,160},{160,192},{192,224},{224... | collective-permute-start | bytes 110600 | tf_op jit(solution)/shard_map/ppermute | solution.py:366
  6.5 1.5 %copy-start = (f32[8,32,128]{2,1,0:T(8,128)S(1)}, f32[8,32,128]{2,1,0:T(8,128)}, u32[]{:S(2)}) copy-start(f32[8,32,128]{2,1,0:T(8,128)} %param.2) | copy-start | bytes 393220
  6.5 5.5 %collective-permute-start.1 = (f32[9,8,128]{2,1,0:T(8,128)S(1)}, f32[9,8,128]{2,1,0:T(8,128)S(1)}, u32[]{:S(2)}, u32[]{:S(2)}) collective-permute-start(f32[9,8,128]{2,1,0:T(8,128)S(1)} %get-tuple-element.7), channel_id=1, source_target_pairs={{32,0},{64,32},{96,64},{128,96},{160,128},{192,160},{224,192},{256... | collective-permute-start | bytes 110600 | tf_op jit(solution)/shard_map/ppermute | solution.py:367
  12.0 5.6 %collective-permute-start.2 = (f32[352,128]{1,0:T(8,128)S(1)}, f32[352,128]{1,0:T(8,128)S(1)}, u32[]{:S(2)}, u32[]{:S(2)}) collective-permute-start(f32[352,128]{1,0:T(8,128)S(1)} %pad_maximum_fusion), channel_id=1, source_target_pairs={{0,1},{1,2},{2,3},{3,4},{4,5},{5,6},{6,7},{7,8},{8,9},{9,10},{10,1... | collective-permute-start | bytes 540680 | tf_op jit(solution)/shard_map/ppermute | solution.py:366
  15.2 6.2 %collective-permute-start.3 = (f32[352,128]{1,0:T(8,128)S(1)}, f32[352,128]{1,0:T(8,128)S(1)}, u32[]{:S(2)}, u32[]{:S(2)}) collective-permute-start(f32[352,128]{1,0:T(8,128)S(1)} %pad_maximum_fusion.1), channel_id=1, source_target_pairs={{1,0},{2,1},{3,2},{4,3},{5,4},{6,5},{7,6},{8,7},{9,8},{10,9},{11,1... | collective-permute-start | bytes 540680 | tf_op jit(solution)/shard_map/ppermute | solution.py:367
  21.5 14.0 %collective-permute-start.4 = (f32[1360,128]{1,0:T(8,128)S(1)}, f32[1360,128]{1,0:T(8,128)S(1)}, u32[]{:S(2)}, u32[]{:S(2)}) collective-permute-start(f32[1360,128]{1,0:T(8,128)S(1)} %constant_dynamic-update-slice_fusion.x), channel_id=1, source_target_pairs={{0,512},{512,0},{1,513},{513,1},{2,514},{514,2},{3,515},{515,3},{4... | collective-permute-start | bytes 2088968 | tf_op jit(solution)/shard_map/ppermute | solution.py:384

commit v3 on v2

--- a/solution.py
+++ b/solution.py
@@ -94,39 +94,65 @@
         to_previous[8, plane : plane + 1] = p_first[plane, 3:4]
 
 
-def assemble(x, k0, dg, slot):
-    def rows_of(at, n):
-        return x[pl.ds(at, n), :]
-
-    k0[slot, 5:13, 8:40] = rows_of(0, 256).reshape(8, 32, 128) * SCALE
-    dg[slot, 4:12, 8:40] = rows_of(256, 256).reshape(8, 32, 128) + FIRST
+def blocks_of(refs):
+    v, p, y_low, y_high, z_low, z_high = refs
+    tiles = [(ref, (plane, pl.ds(8 * r, 8))) for ref in (v, p) for plane in range(8) for r in range(4)]
+    tiles += [(ref, (plane, pl.ds(0, 8))) for ref in (y_low, y_high) for plane in range(9)]
+    return tiles + [(ref, (pl.ds(8 * r, 8),)) for ref in (z_low, z_high) for r in range(44)]
+
+
+def side_kernel(*refs):
+    out = refs[-1]
+    mine = lax.axis_index("slab")
+    lane = lanes()
+    tiles = blocks_of(refs[:-1])
+    for start in range(0, len(tiles), 16):
+        packed = jnp.zeros((8, 128), jnp.float32)
+        for k, (ref, at) in enumerate(tiles[start : start + 16]):
+            moved = pltpu.roll(ref[at], lax.rem(8 * k + 8 * (1 - mine), 128), 1)
+            packed = jnp.where((lane >= 8 * k) & (lane < 8 * k + 8), moved, packed)
+        out[start // 2 : start // 2 + 8] = packed
+
+
+def assemble(tile_of, k0, dg, slot):
     row = lax.broadcasted_iota(jnp.int32, (8, 128), 0)
 
-    def halo(at, high, plane, fourth=None):
-        tile = rows_of(at, 8)
+    def halo(tile, high, plane, fourth=None):
         rows = slice(40, 48) if high else slice(0, 8)
         k0[slot, plane, rows] = tile * SCALE
         near = pltpu.roll(tile, 3 if high else 5, 0)
         if fourth is not None:
-            far = jnp.broadcast_to(x[pl.ds(fourth, 1), :], (8, 128))
-            near = jnp.where(row == (3 if high else 4), far, near)
+            near = jnp.where(row == (3 if high else 4), jnp.broadcast_to(fourth, (8, 128)), near)
         dg[slot, plane - 1, rows] = near + FIRST
 
+    def inner(ref, plane, r, value):
+        ref[slot, plane, 8 + 8 * r : 16 + 8 * r] = value
+
+    for plane in range(8):
+        for r in range(4):
+            inner(k0, 5 + plane, r, tile_of(4 * plane + r) * SCALE)
+            inner(dg, 4 + plane, r, tile_of(32 + 4 * plane + r) + FIRST)
     for high in (0, 1):
-        start = 512 + 72 * high
+        start = 64 + 9 * high
+        fourths = tile_of(start + 8)
         for plane in range(8):
-            halo(start + 8 * plane, high, 5 + plane, start + 64 + plane)
+            halo(tile_of(start + plane), high, 5 + plane, fourths[plane : plane + 1])
     for side in (0, 1):
-        start = 656 + 352 * side
-        own, at = (13, 12) if side else (0, 0)
-        k0[slot, own : own + 5, 8:40] = rows_of(start, 160).reshape(5, 32, 128) * SCALE
-        dg[slot, at : at + 4, 8:40] = rows_of(start + 160, 128).reshape(4, 32, 128) + FIRST
+        start = 82 + 44 * side
+        for plane in range(5):
+            for r in range(4):
+                inner(k0, (13 if side else 0) + plane, r, tile_of(start + 4 * plane + r) * SCALE)
+        for plane in range(4):
+            for r in range(4):
+                value = tile_of(start + 20 + 4 * plane + r) + FIRST
+                inner(dg, (12 if side else 0) + plane, r, value)
         for high in (0, 1):
             for plane in range(4):
-                halo(start + 288 + 32 * high + 8 * plane, high, (13 if side else 1) + plane)
-
-
-def krylov_kernel(x, q, k_out, row_out, k0, k1, k2, k3, k4, k5, dg):
+                tile = tile_of(start + 36 + 4 * high + plane)
+                halo(tile, high, (13 if side else 1) + plane)
+
+
+def krylov_kernel(v, p, y_low, y_high, z_low, z_high, side, k_out, row_out, k0, k1, k2, k3, k4, k5, dg):
     mine = lax.axis_index("slab")
     y, z = lax.axis_index("py"), lax.axis_index("pz")
     inside = {
@@ -135,27 +161,40 @@
         "z_low": jnp.where(z > 0, 1.0, 0.0),
         "z_high": jnp.where(z < lax.axis_size("pz") - 1, 1.0, 0.0),
     }
-    assemble(x, k0, dg, mine)
-    assemble(q, k0, dg, 1 - mine)
     lane = lax.broadcasted_iota(jnp.int32, (48, 128), 1)
     first, last = lane == 0, lane == 127
+    near = (lane >= 120 * mine) & (lane < 8 + 120 * mine)
+    near8 = near[0:8]
+    tiles = blocks_of((v, p, y_low, y_high, z_low, z_high))
+
+    def own_tile(n):
+        ref, at = tiles[n]
+        return ref[at]
+
+    def other_tile(n):
+        k = n % 16
+        shift = lax.rem(120 * mine + 128 - 8 * k, 128)
+        return jnp.where(near8, pltpu.roll(side[pl.ds(n // 16 * 8, 8), :], shift, 1), 0.0)
+
+    assemble(own_tile, k0, dg, 0)
+    assemble(other_tile, k0, dg, 1)
     basis = (k0, k1, k2, k3, k4, k5)
     for step in range(1, COUNT):
         old, new = basis[step - 1], basis[step]
         shift = SHIFTS[0] - SHIFTS[step - 1]
         for plane in range(step, 18 - step):
+            away = max(5 - plane, plane - 12, 0)
             f = [old[t, plane] for t in (0, 1)]
             up = [pltpu.roll(a, 1, 1) for a in f]
             down = [pltpu.roll(a, 127, 1) for a in f]
-            beside = [
-                jnp.where(first, 0.0, up[0]) + jnp.where(last, down[1], down[0]),
-                jnp.where(first, up[0], up[1]) + jnp.where(last, 0.0, down[1]),
-            ]
-            outer = step == ITERS or plane in (step, 17 - step)
-            rows = slice(8, 40) if outer else slice(0, 48)
             for t in (0, 1):
+                reach = ITERS - step - t - away
+                if reach < 0:
+                    continue
+                beside = jnp.where(first, up[1 - t], up[t]) + jnp.where(last, down[1 - t], down[t])
+                rows = slice(0, 48) if reach > 0 else slice(8, 40)
                 along_y = old[t, plane, 7:39] + old[t, plane, 9:41]
-                if not outer:
+                if reach > 0:
                     along_y = jnp.concatenate(
                         [
                             pltpu.roll(f[t][0:8], 1, 0) + old[t, plane, 1:9],
@@ -163,20 +202,22 @@
                             old[t, plane, 39:47] + pltpu.roll(f[t][40:48], 7, 0),
                         ]
                     )
-                around = beside[t][rows] + along_y
+                around = beside[rows] + along_y
                 around = around + (old[t, plane - 1, rows] + old[t, plane + 1, rows])
                 factor = dg[t, plane - 1, rows]
                 if shift != 0.0:
                     factor = factor + shift
                 image = factor * f[t][rows] - around
+                if t == 1:
+                    image = jnp.where(near[rows], image, 0.0)
                 if step == ITERS:
-                    new[t, plane - ITERS] = image
+                    new[plane - ITERS] = image
                     continue
                 if plane < ITERS:
                     image = image * inside["z_low"]
                 if plane >= 13:
                     image = image * inside["z_high"]
-                if outer:
+                if reach == 0:
                     new[t, plane, rows] = image
                     continue
                 new[t, plane, 0:8] = image[0:8] * inside["y_low"]
@@ -185,8 +226,8 @@
     sums = [None] * len(PAIRS)
     for plane in range(8):
         for tile in range(4):
-            own = [b[mine, 5 + plane, 8 + 8 * tile : 16 + 8 * tile] for b in basis[:ITERS]]
-            own.append(k5[mine, plane, 8 * tile : 8 + 8 * tile])
+            own = [b[0, 5 + plane, 8 + 8 * tile : 16 + 8 * tile] for b in basis[:ITERS]]
+            own.append(k5[plane, 8 * tile : 8 + 8 * tile])
             for i, value in enumerate(own):
                 k_out[i, plane, 8 * tile : 8 + 8 * tile] = value
             parts = [split(value) for value in own]
@@ -293,7 +334,7 @@
     return alphas, betas
 
 
-def lanczos_kernel(per_cell, rows, basis, vectors, tridiagonal, made, done):
+def lanczos_kernel(per_cell, rows, basis, vectors, tridiagonal, made, small, done):
     total = sum_of_rows(rows)
     lane, row = lanes(), lax.broadcasted_iota(jnp.int32, (8, 128), 0)
     gram = []
@@ -331,9 +372,12 @@
         table = jnp.zeros((8, 128), jnp.float32)
         for j, value in enumerate(values):
             table = jnp.where(lane == j, value, table)
-        tridiagonal[r : r + 1, :] = table[0:1, 0:ITERS]
+        small[r : r + 1, :] = table[0:1, 0:ITERS]
+    last = pltpu.make_async_copy(small, tridiagonal, done.at[COUNT])
+    last.start()
     for j in range(COUNT):
         copy(j).wait()
+    last.wait()
 
 
 def call(kernel, out_shape, scratch=(), flops=10000, mebibytes=4, **specs):
@@ -380,18 +424,19 @@
         to_rows(v[:5], p[:4], y_low[:4], y_high[:4]),
         "pz",
     )
-    x = to_rows(v, p, y_low, y_high, z_low, z_high)
-    q = lax.ppermute(x, "slab", [(0, 1), (1, 0)])
+    blocks = (v, p, y_low, y_high, z_low, z_high)
+    side = call(side_kernel, jax.ShapeDtypeStruct((88, 128), f32))(*blocks)
+    side = lax.ppermute(side, "slab", [(0, 1), (1, 0)])
     n_z = lax.axis_size("pz")
     n_xy = lax.axis_size("slab") * lax.axis_size("py")
     block = [pltpu.VMEM((2, 18, 48, 128), f32)] * 5
     basis, rows = call(
         krylov_kernel,
         (jax.ShapeDtypeStruct((COUNT, 8, 32, 128), f32), jax.ShapeDtypeStruct((n_z, 128), f32)),
-        block + [pltpu.VMEM((2, 8, 32, 128), f32), pltpu.VMEM((2, 16, 48, 128), f32)],
+        block + [pltpu.VMEM((8, 32, 128), f32), pltpu.VMEM((2, 16, 48, 128), f32)],
         20000000,
         12,
-    )(x, q)
+    )(*blocks, side)
     rows = lax.all_to_all(rows, "pz", 0, 0, tiled=True)
     rows = call(rows_kernel, jax.ShapeDtypeStruct((n_xy, 128), f32))(rows)
     rows = lax.all_to_all(rows, ("slab", "py"), 0, 0, tiled=True)
@@ -402,12 +447,13 @@
             jax.ShapeDtypeStruct((COUNT, 8, 32, 128), f32),
             jax.ShapeDtypeStruct((2, ITERS), f32),
         ),
-        [pltpu.VMEM((COUNT, 8, 32, 128), f32), pltpu.SemaphoreType.DMA((COUNT,))],
+        [
+            pltpu.VMEM((COUNT, 8, 32, 128), f32),
+            pltpu.VMEM((2, ITERS), f32),
+            pltpu.SemaphoreType.DMA((COUNT + 1,)),
+        ],
         flops=20000000,
-        out_specs=(
-            pl.BlockSpec(memory_space=pl.ANY),
-            pl.BlockSpec(memory_space=pltpu.VMEM),
-        ),
+        out_specs=(pl.BlockSpec(memory_space=pl.ANY),) * 2,
     )(rows, basis)
 
 

time: 85.1 us -> 83.6 us (0.982)
    ppermute x1, waiting for transfers between devices: 1.76 us -> 0.85 us  [shards(): side = lax.ppermute(side, 'slab', [(0, 1), (1, 0)])]
where the time goes in v3:
time: 83.6 us; the launch traced here: 83.2 us
  blocking collectives  43.7 us (52%)
  starting transfers between devices  23.1 us (28%)
  waiting for transfers between devices  9.75 us (12%)
  Pallas kernels  5.03 us (6%)
  local copies, waits for them, and re-layouts  0.87 us (1%)
    all_to_all x1, blocking collectives, shards(): rows = lax.all_to_all(rows, ('slab', 'py'), 0, 0, tiled=True)  32 us
    ppermute x1, starting transfers between devices, shards(): side = lax.ppermute(side, 'slab', [(0, 1), (1, 0)])  12.2 us
    all_to_all x1, blocking collectives, shards(): rows = lax.all_to_all(rows, 'pz', 0, 0, tiled=True)  11.6 us
    ppermute x2, starting transfers between devices, exchange(): lax.ppermute(to_next, axis, line(axis, 1))  8.16 us
    ppermute x2, waiting for transfers between devices, exchange(): lax.ppermute(to_previous, axis, line(axis, -1))  7.81 us
    pallas_call x1, Pallas kernels, shards(): call(krylov_kernel, (jax.ShapeDtypeStruct((COUNT, 8, 32, 128), f32), jax....  2.86 us
    ppermute x2, starting transfers between devices, exchange(): lax.ppermute(to_previous, axis, line(axis, -1))  2.72 us
    pallas_call x1, Pallas kernels, shards(): call(functools.partial(lanczos_kernel, per_cell), (jax.ShapeDtypeStruct((...  1.73 us
  transfers between devices with their start and end apart: 5, of which 4 were waited for; matrix products, arithmetic and copies ran while one was open for 0% of the time, Pallas kernels for 0%

profile of v3, /device:TPU:1, one launch (start us, length us, event | category | flops | bytes accessed | tf_op | source)
XLA Modules:
  0.0 83.2 jit_solution(8416788460918060327)
XLA Ops:
  0.6 0.8 fusion.2
  1.5 0.0 copy-start
  1.5 4.9 %collective-permute-start = (f32[9,8,128]{2,1,0:T(8,128)S(1)}, f32[9,8,128]{2,1,0:T(8,128)S(1)}, u32[]{:S(2)}, u32[]{:S(2)}) collective-permute-start(f32[9,8,128]{2,1,0:T(8,128)S(1)} %get-tuple-element.6), channel_id=1, source_target_pairs={{0,32},{32,64},{64,96},{96,128},{128,160},{160,192},{192,224},{224... | collective-permute-start | bytes 110600 | tf_op jit(solution)/shard_map/ppermute | solution.py:410
  6.5 0.0 copy-start.1
  6.5 1.4 %collective-permute-start.1 = (f32[9,8,128]{2,1,0:T(8,128)S(1)}, f32[9,8,128]{2,1,0:T(8,128)S(1)}, u32[]{:S(2)}, u32[]{:S(2)}) collective-permute-start(f32[9,8,128]{2,1,0:T(8,128)S(1)} %get-tuple-element.7), channel_id=1, source_target_pairs={{32,0},{64,32},{96,64},{128,96},{160,128},{192,160},{224,192},{256... | collective-permute-start | bytes 110600 | tf_op jit(solution)/shard_map/ppermute | solution.py:411
  7.9 0.0 copy-done
  7.9 0.0 copy-done.1
  8.0 0.0 collective-permute-done.refs_2_.y_low
  8.0 4.0 %collective-permute-done.1.refs_3_.y_high = f32[9,8,128]{2,1,0:T(8,128)S(1)} collective-permute-done((f32[9,8,128]{2,1,0:T(8,128)S(1)}, f32[9,8,128]{2,1,0:T(8,128)S(1)}, u32[]{:S(2)}, u32[]{:S(2)}) %collective-permute-start.1) | collective-permute-done | bytes 36896 | tf_op jit(solution)/shard_map/ppermute | solution.py:411
  12.0 3.2 %collective-permute-start.2 = (f32[352,128]{1,0:T(8,128)S(1)}, f32[352,128]{1,0:T(8,128)S(1)}, u32[]{:S(2)}, u32[]{:S(2)}) collective-permute-start(f32[352,128]{1,0:T(8,128)S(1)} %pad_maximum_fusion), channel_id=1, source_target_pairs={{0,1},{1,2},{2,3},{3,4},{4,5},{5,6},{6,7},{7,8},{8,9},{9,10},{10,1... | collective-permute-start | bytes 540680 | tf_op jit(solution)/shard_map/ppermute | solution.py:410
  15.2 1.3 %collective-permute-start.3 = (f32[352,128]{1,0:T(8,128)S(1)}, f32[352,128]{1,0:T(8,128)S(1)}, u32[]{:S(2)}, u32[]{:S(2)}) collective-permute-start(f32[352,128]{1,0:T(8,128)S(1)} %pad_maximum_fusion.1), channel_id=1, source_target_pairs={{1,0},{2,1},{3,2},{4,3},{5,4},{6,5},{7,6},{8,7},{9,8},{10,9},{11,1... | collective-permute-start | bytes 540680 | tf_op jit(solution)/shard_map/ppermute | solution.py:411
  16.5 1.1 %collective-permute-done.2.refs_4_.z_low = f32[352,128]{1,0:T(8,128)S(1)} collective-permute-done((f32[352,128]{1,0:T(8,128)S(1)}, f32[352,128]{1,0:T(8,128)S(1)}, u32[]{:S(2)}, u32[]{:S(2)}) %collective-permute-start.2) | collective-permute-done | bytes 180256 | tf_op jit(solution)/shard_map/ppermute | solution.py:410
  17.6 3.9 %collective-permute-done.3.refs_5_.z_high = f32[352,128]{1,0:T(8,128)S(1)} collective-permute-done((f32[352,128]{1,0:T(8,128)S(1)}, f32[352,128]{1,0:T(8,128)S(1)}, u32[]{:S(2)}, u32[]{:S(2)}) %collective-permute-start.3) | collective-permute-done | bytes 180256 | tf_op jit(solution)/shard_map/ppermute | solution.py:411
  21.4 0.3 shard_map.42
  21.7 12.2 %collective-permute-start.4 = (f32[88,128]{1,0:T(8,128)S(1)}, f32[88,128]{1,0:T(8,128)S(1)}, u32[]{:S(2)}, u32[]{:S(2)}) collective-permute-start(f32[88,128]{1,0:T(8,128)S(1)} %shard_map.42), channel_id=1, source_target_pairs={{0,512},{512,0},{1,513},{513,1},{2,514},{514,2},{3,515},{515,3},{4... | collective-permute-start | bytes 135176 | tf_op jit(solution)/shard_map/ppermute | solution.py:429
  34.0 0.9 %collective-permute-done.4.side = f32[88,128]{1,0:T(8,128)S(1)} collective-permute-done((f32[88,128]{1,0:T(8,128)S(1)}, f32[88,128]{1,0:T(8,128)S(1)}, u32[]{:S(2)}, u32[]{:S(2)}) %collective-permute-start.4) | collective-permute-done | bytes 45088 | tf_op jit(solution)/shard_map/ppermute | solution.py:429
  34.8 2.9 %shard_map.43 = (f32[6,8,32,128]{3,2,1,0:T(8,128)S(1)}, f32[32,128]{1,0:T(8,128)S(1)}) custom-call(f32[8,32,128]{2,1,0:T(8,128)S(1)} %copy-done, f32[8,32,128]{2,1,0:T(8,128)S(1)} %copy-done.1, f32[9,8,128]{2,1,0:T(8,128)S(1)} %collective-permute-done.refs_2_.y_low, f32[9,8,128]{2,1,0:T(8,128)S(1)} %collective-permute-done.1.refs_3_.y_high, ...), custom_call_target="tpu_custom_call" | custom-call | flops 20000000 | bytes 20000000 | tf_op jit(solution)/shard_map/pallas_call | solution.py:433
  37.7 11.6 %all_to_all.22 = f32[32,1,128]{2,1,0:T(1,128)S(1)} all-to-all(f32[32,1,128]{2,1,0:T(1,128)S(1)} %bitcast.23), channel_id=1, replica_groups=mesh['slab'=2,'py'=16,'pz'=32] {'pz'}, dimensions={0} | all-to-all | bytes 32768 | tf_op jit(solution)/shard_map/all_to_all | solution.py:440
  49.3 0.2 shard_map.44
  49.5 32.0 %all_to_all.23 = f32[32,1,128]{2,1,0:T(1,128)S(1)} all-to-all(f32[32,1,128]{2,1,0:T(1,128)S(1)} %bitcast.22), channel_id=1, replica_groups=mesh['slab'=2,'py'=16,'pz'=32] {'slab','py'}, dimensions={0} | all-to-all | bytes 32768 | tf_op jit(solution)/shard_map/all_to_all | solution.py:442
  81.5 1.7 %shard_map.45 = (f32[6,8,32,128]{3,2,1,0:T(8,128)}, f32[2,5]{1,0:T(2,128)}) custom-call(f32[32,128]{1,0:T(8,128)S(1)} %bitcast.20, f32[6,8,32,128]{3,2,1,0:T(8,128)S(1)} %get-tuple-element.9.basis), custom_call_target="tpu_custom_call" | custom-call | flops 20000000 | bytes 20000000 | tf_op jit(solution)/shard_map/pallas_call | solution.py:444
  (7 shorter events, 0.1 us)
Async XLA Ops:
  1.5 6.4 %copy-start = (f32[8,32,128]{2,1,0:T(8,128)S(1)}, f32[8,32,128]{2,1,0:T(8,128)}, u32[]{:S(2)}) copy-start(f32[8,32,128]{2,1,0:T(8,128)} %v.1) | copy-start | bytes 393220
  1.5 6.5 %collective-permute-start = (f32[9,8,128]{2,1,0:T(8,128)S(1)}, f32[9,8,128]{2,1,0:T(8,128)S(1)}, u32[]{:S(2)}, u32[]{:S(2)}) collective-permute-start(f32[9,8,128]{2,1,0:T(8,128)S(1)} %get-tuple-element.6), channel_id=1, source_target_pairs={{0,32},{32,64},{64,96},{96,128},{128,160},{160,192},{192,224},{224... | collective-permute-start | bytes 110600 | tf_op jit(solution)/shard_map/ppermute | solution.py:410
  6.5 1.5 %copy-start.1 = (f32[8,32,128]{2,1,0:T(8,128)S(1)}, f32[8,32,128]{2,1,0:T(8,128)}, u32[]{:S(2)}) copy-start(f32[8,32,128]{2,1,0:T(8,128)} %p.1) | copy-start | bytes 393220
  6.5 5.5 %collective-permute-start.1 = (f32[9,8,128]{2,1,0:T(8,128)S(1)}, f32[9,8,128]{2,1,0:T(8,128)S(1)}, u32[]{:S(2)}, u32[]{:S(2)}) collective-permute-start(f32[9,8,128]{2,1,0:T(8,128)S(1)} %get-tuple-element.7), channel_id=1, source_target_pairs={{32,0},{64,32},{96,64},{128,96},{160,128},{192,160},{224,192},{256... | collective-permute-start | bytes 110600 | tf_op jit(solution)/shard_map/ppermute | solution.py:411
  12.0 5.6 %collective-permute-start.2 = (f32[352,128]{1,0:T(8,128)S(1)}, f32[352,128]{1,0:T(8,128)S(1)}, u32[]{:S(2)}, u32[]{:S(2)}) collective-permute-start(f32[352,128]{1,0:T(8,128)S(1)} %pad_maximum_fusion), channel_id=1, source_target_pairs={{0,1},{1,2},{2,3},{3,4},{4,5},{5,6},{6,7},{7,8},{8,9},{9,10},{10,1... | collective-permute-start | bytes 540680 | tf_op jit(solution)/shard_map/ppermute | solution.py:410
  15.2 6.2 %collective-permute-start.3 = (f32[352,128]{1,0:T(8,128)S(1)}, f32[352,128]{1,0:T(8,128)S(1)}, u32[]{:S(2)}, u32[]{:S(2)}) collective-permute-start(f32[352,128]{1,0:T(8,128)S(1)} %pad_maximum_fusion.1), channel_id=1, source_target_pairs={{1,0},{2,1},{3,2},{4,3},{5,4},{6,5},{7,6},{8,7},{9,8},{10,9},{11,1... | collective-permute-start | bytes 540680 | tf_op jit(solution)/shard_map/ppermute | solution.py:411
  21.7 13.1 %collective-permute-start.4 = (f32[88,128]{1,0:T(8,128)S(1)}, f32[88,128]{1,0:T(8,128)S(1)}, u32[]{:S(2)}, u32[]{:S(2)}) collective-permute-start(f32[88,128]{1,0:T(8,128)S(1)} %shard_map.42), channel_id=1, source_target_pairs={{0,512},{512,0},{1,513},{513,1},{2,514},{514,2},{3,515},{515,3},{4... | collective-permute-start | bytes 135176 | tf_op jit(solution)/shard_map/ppermute | solution.py:429

commit v4 on v3

--- a/solution.py
+++ b/solution.py
@@ -11,7 +11,7 @@
 EPSILON = 1e-06
 INTERPRET = False
 
-SHIFTS = (2.25, 14.25, 8.25, 2.25, 14.25)
+SHIFTS = (1.25, 3.25, 8.25, 14.25, 4.25)
 SCALE = 2.0**24
 FIRST = 6.0 - SHIFTS[0]
 COUNT = ITERS + 1
@@ -432,14 +432,14 @@
     block = [pltpu.VMEM((2, 18, 48, 128), f32)] * 5
     basis, rows = call(
         krylov_kernel,
-        (jax.ShapeDtypeStruct((COUNT, 8, 32, 128), f32), jax.ShapeDtypeStruct((n_z, 128), f32)),
+        (jax.ShapeDtypeStruct((COUNT, 8, 32, 128), f32), jax.ShapeDtypeStruct((n_xy, 128), f32)),
         block + [pltpu.VMEM((8, 32, 128), f32), pltpu.VMEM((2, 16, 48, 128), f32)],
         20000000,
         12,
     )(*blocks, side)
+    rows = lax.all_to_all(rows, ("slab", "py"), 0, 0, tiled=True)
+    rows = call(rows_kernel, jax.ShapeDtypeStruct((n_z, 128), f32))(rows)
     rows = lax.all_to_all(rows, "pz", 0, 0, tiled=True)
-    rows = call(rows_kernel, jax.ShapeDtypeStruct((n_xy, 128), f32))(rows)
-    rows = lax.all_to_all(rows, ("slab", "py"), 0, 0, tiled=True)
     per_cell = 1.0 / (v.size * n_z * n_xy)
     return call(
         functools.partial(lanczos_kernel, per_cell),

time: 83.6 us -> 82.2 us (0.983)
  blocking collectives: 43.7 us -> 42.2 us
    all_to_all x1, blocking collectives: 32 us -> 23.9 us  [shards(): rows = lax.all_to_all(rows, ('slab', 'py'), 0, 0, tiled=True)]
    all_to_all x1, blocking collectives: 11.6 us -> 18.3 us  [shards(): rows = lax.all_to_all(rows, 'pz', 0, 0, tiled=True)]
where the time goes in v4:
time: 82.2 us; the launch traced here: 81.8 us
  blocking collectives  42.2 us (51%)
  starting transfers between devices  23.1 us (28%)
  waiting for transfers between devices  9.75 us (12%)
  Pallas kernels  5.05 us (6%)
  local copies, waits for them, and re-layouts  0.87 us (1%)
    all_to_all x1, blocking collectives, shards(): rows = lax.all_to_all(rows, ('slab', 'py'), 0, 0, tiled=True)  23.9 us
    all_to_all x1, blocking collectives, shards(): rows = lax.all_to_all(rows, 'pz', 0, 0, tiled=True)  18.3 us
    ppermute x1, starting transfers between devices, shards(): side = lax.ppermute(side, 'slab', [(0, 1), (1, 0)])  12.2 us
    ppermute x2, starting transfers between devices, exchange(): lax.ppermute(to_next, axis, line(axis, 1))  8.16 us
    ppermute x2, waiting for transfers between devices, exchange(): lax.ppermute(to_previous, axis, line(axis, -1))  7.81 us
    pallas_call x1, Pallas kernels, shards(): call(krylov_kernel, (jax.ShapeDtypeStruct((COUNT, 8, 32, 128), f32), jax....  2.87 us
    ppermute x2, starting transfers between devices, exchange(): lax.ppermute(to_previous, axis, line(axis, -1))  2.72 us
    pallas_call x1, Pallas kernels, shards(): call(functools.partial(lanczos_kernel, per_cell), (jax.ShapeDtypeStruct((...  1.73 us
  transfers between devices with their start and end apart: 5, of which 4 were waited for; matrix products, arithmetic and copies ran while one was open for 0% of the time, Pallas kernels for 0%

profile of v4, /device:TPU:1, one launch (start us, length us, event | category | flops | bytes accessed | tf_op | source)
XLA Modules:
  0.0 81.8 jit_solution(11444080437941041846)
XLA Ops:
  0.6 0.8 %fusion.2 = (f32[8,8,128]{2,1,0:T(8,128)S(1)}, f32[8,8,128]{2,1,0:T(8,128)S(1)}, f32[8,8,128]{2,1,0:T(8,128)S(1)}, f32[8,8,128]{2,1,0:T(8,128)S(1)}) fusion(f32[8,32,128]{2,1,0:T(8,128)} %p.1, f32[8,32,128]{2,1,0:T(8,128)} %v.1), kind=kLoop, calls=%fused_computation.8 | loop fusion | bytes 262144 | tf_op jit(solution)/shard_map/slice | solution.py:418
  1.5 0.0 copy-start
  1.5 4.9 %collective-permute-start = (f32[9,8,128]{2,1,0:T(8,128)S(1)}, f32[9,8,128]{2,1,0:T(8,128)S(1)}, u32[]{:S(2)}, u32[]{:S(2)}) collective-permute-start(f32[9,8,128]{2,1,0:T(8,128)S(1)} %get-tuple-element.6), channel_id=1, source_target_pairs={{0,32},{32,64},{64,96},{96,128},{128,160},{160,192},{192,224},{224... | collective-permute-start | bytes 110600 | tf_op jit(solution)/shard_map/ppermute | solution.py:410
  6.5 0.0 copy-start.1
  6.5 1.4 %collective-permute-start.1 = (f32[9,8,128]{2,1,0:T(8,128)S(1)}, f32[9,8,128]{2,1,0:T(8,128)S(1)}, u32[]{:S(2)}, u32[]{:S(2)}) collective-permute-start(f32[9,8,128]{2,1,0:T(8,128)S(1)} %get-tuple-element.7), channel_id=1, source_target_pairs={{32,0},{64,32},{96,64},{128,96},{160,128},{192,160},{224,192},{256... | collective-permute-start | bytes 110600 | tf_op jit(solution)/shard_map/ppermute | solution.py:411
  7.9 0.0 copy-done
  7.9 0.0 copy-done.1
  8.0 0.0 collective-permute-done.refs_2_.y_low
  8.0 4.0 %collective-permute-done.1.refs_3_.y_high = f32[9,8,128]{2,1,0:T(8,128)S(1)} collective-permute-done((f32[9,8,128]{2,1,0:T(8,128)S(1)}, f32[9,8,128]{2,1,0:T(8,128)S(1)}, u32[]{:S(2)}, u32[]{:S(2)}) %collective-permute-start.1) | collective-permute-done | bytes 36896 | tf_op jit(solution)/shard_map/ppermute | solution.py:411
  12.0 3.2 %collective-permute-start.2 = (f32[352,128]{1,0:T(8,128)S(1)}, f32[352,128]{1,0:T(8,128)S(1)}, u32[]{:S(2)}, u32[]{:S(2)}) collective-permute-start(f32[352,128]{1,0:T(8,128)S(1)} %pad_maximum_fusion), channel_id=1, source_target_pairs={{0,1},{1,2},{2,3},{3,4},{4,5},{5,6},{6,7},{7,8},{8,9},{9,10},{10,1... | collective-permute-start | bytes 540680 | tf_op jit(solution)/shard_map/ppermute | solution.py:410
  15.2 1.3 %collective-permute-start.3 = (f32[352,128]{1,0:T(8,128)S(1)}, f32[352,128]{1,0:T(8,128)S(1)}, u32[]{:S(2)}, u32[]{:S(2)}) collective-permute-start(f32[352,128]{1,0:T(8,128)S(1)} %pad_maximum_fusion.1), channel_id=1, source_target_pairs={{1,0},{2,1},{3,2},{4,3},{5,4},{6,5},{7,6},{8,7},{9,8},{10,9},{11,1... | collective-permute-start | bytes 540680 | tf_op jit(solution)/shard_map/ppermute | solution.py:411
  16.5 1.1 %collective-permute-done.2.refs_4_.z_low = f32[352,128]{1,0:T(8,128)S(1)} collective-permute-done((f32[352,128]{1,0:T(8,128)S(1)}, f32[352,128]{1,0:T(8,128)S(1)}, u32[]{:S(2)}, u32[]{:S(2)}) %collective-permute-start.2) | collective-permute-done | bytes 180256 | tf_op jit(solution)/shard_map/ppermute | solution.py:410
  17.6 3.9 %collective-permute-done.3.refs_5_.z_high = f32[352,128]{1,0:T(8,128)S(1)} collective-permute-done((f32[352,128]{1,0:T(8,128)S(1)}, f32[352,128]{1,0:T(8,128)S(1)}, u32[]{:S(2)}, u32[]{:S(2)}) %collective-permute-start.3) | collective-permute-done | bytes 180256 | tf_op jit(solution)/shard_map/ppermute | solution.py:411
  21.4 0.3 shard_map.42
  21.7 12.2 %collective-permute-start.4 = (f32[88,128]{1,0:T(8,128)S(1)}, f32[88,128]{1,0:T(8,128)S(1)}, u32[]{:S(2)}, u32[]{:S(2)}) collective-permute-start(f32[88,128]{1,0:T(8,128)S(1)} %shard_map.42), channel_id=1, source_target_pairs={{0,512},{512,0},{1,513},{513,1},{2,514},{514,2},{3,515},{515,3},{4... | collective-permute-start | bytes 135176 | tf_op jit(solution)/shard_map/ppermute | solution.py:429
  34.0 0.9 %collective-permute-done.4.side = f32[88,128]{1,0:T(8,128)S(1)} collective-permute-done((f32[88,128]{1,0:T(8,128)S(1)}, f32[88,128]{1,0:T(8,128)S(1)}, u32[]{:S(2)}, u32[]{:S(2)}) %collective-permute-start.4) | collective-permute-done | bytes 45088 | tf_op jit(solution)/shard_map/ppermute | solution.py:429
  34.8 2.9 %shard_map.43 = (f32[6,8,32,128]{3,2,1,0:T(8,128)S(1)}, f32[32,128]{1,0:T(8,128)S(1)}) custom-call(f32[8,32,128]{2,1,0:T(8,128)S(1)} %copy-done, f32[8,32,128]{2,1,0:T(8,128)S(1)} %copy-done.1, f32[9,8,128]{2,1,0:T(8,128)S(1)} %collective-permute-done.refs_2_.y_low, f32[9,8,128]{2,1,0:T(8,128)S(1)} %collective-permute-done.1.refs_3_.y_high, ...), custom_call_target="tpu_custom_call" | custom-call | flops 20000000 | bytes 20000000 | tf_op jit(solution)/shard_map/pallas_call | solution.py:433
  37.7 23.9 %all_to_all.22 = f32[32,1,128]{2,1,0:T(1,128)S(1)} all-to-all(f32[32,1,128]{2,1,0:T(1,128)S(1)} %bitcast.23), channel_id=1, replica_groups=mesh['slab'=2,'py'=16,'pz'=32] {'slab','py'}, dimensions={0} | all-to-all | bytes 32768 | tf_op jit(solution)/shard_map/all_to_all | solution.py:440
  61.6 0.2 shard_map.44
  61.8 18.3 %all_to_all.23 = f32[32,1,128]{2,1,0:T(1,128)S(1)} all-to-all(f32[32,1,128]{2,1,0:T(1,128)S(1)} %bitcast.22), channel_id=1, replica_groups=mesh['slab'=2,'py'=16,'pz'=32] {'pz'}, dimensions={0} | all-to-all | bytes 32768 | tf_op jit(solution)/shard_map/all_to_all | solution.py:442
  80.1 1.7 %shard_map.45 = (f32[6,8,32,128]{3,2,1,0:T(8,128)}, f32[2,5]{1,0:T(2,128)}) custom-call(f32[32,128]{1,0:T(8,128)S(1)} %bitcast.20, f32[6,8,32,128]{3,2,1,0:T(8,128)S(1)} %get-tuple-element.9.basis), custom_call_target="tpu_custom_call" | custom-call | flops 20000000 | bytes 20000000 | tf_op jit(solution)/shard_map/pallas_call | solution.py:444
  (7 shorter events, 0.1 us)
Async XLA Ops:
  1.5 6.4 %copy-start = (f32[8,32,128]{2,1,0:T(8,128)S(1)}, f32[8,32,128]{2,1,0:T(8,128)}, u32[]{:S(2)}) copy-start(f32[8,32,128]{2,1,0:T(8,128)} %v.1) | copy-start | bytes 393220
  1.5 6.5 %collective-permute-start = (f32[9,8,128]{2,1,0:T(8,128)S(1)}, f32[9,8,128]{2,1,0:T(8,128)S(1)}, u32[]{:S(2)}, u32[]{:S(2)}) collective-permute-start(f32[9,8,128]{2,1,0:T(8,128)S(1)} %get-tuple-element.6), channel_id=1, source_target_pairs={{0,32},{32,64},{64,96},{96,128},{128,160},{160,192},{192,224},{224... | collective-permute-start | bytes 110600 | tf_op jit(solution)/shard_map/ppermute | solution.py:410
  6.5 1.5 %copy-start.1 = (f32[8,32,128]{2,1,0:T(8,128)S(1)}, f32[8,32,128]{2,1,0:T(8,128)}, u32[]{:S(2)}) copy-start(f32[8,32,128]{2,1,0:T(8,128)} %p.1) | copy-start | bytes 393220
  6.5 5.5 %collective-permute-start.1 = (f32[9,8,128]{2,1,0:T(8,128)S(1)}, f32[9,8,128]{2,1,0:T(8,128)S(1)}, u32[]{:S(2)}, u32[]{:S(2)}) collective-permute-start(f32[9,8,128]{2,1,0:T(8,128)S(1)} %get-tuple-element.7), channel_id=1, source_target_pairs={{32,0},{64,32},{96,64},{128,96},{160,128},{192,160},{224,192},{256... | collective-permute-start | bytes 110600 | tf_op jit(solution)/shard_map/ppermute | solution.py:411
  12.0 5.6 %collective-permute-start.2 = (f32[352,128]{1,0:T(8,128)S(1)}, f32[352,128]{1,0:T(8,128)S(1)}, u32[]{:S(2)}, u32[]{:S(2)}) collective-permute-start(f32[352,128]{1,0:T(8,128)S(1)} %pad_maximum_fusion), channel_id=1, source_target_pairs={{0,1},{1,2},{2,3},{3,4},{4,5},{5,6},{6,7},{7,8},{8,9},{9,10},{10,1... | collective-permute-start | bytes 540680 | tf_op jit(solution)/shard_map/ppermute | solution.py:410
  15.2 6.2 %collective-permute-start.3 = (f32[352,128]{1,0:T(8,128)S(1)}, f32[352,128]{1,0:T(8,128)S(1)}, u32[]{:S(2)}, u32[]{:S(2)}) collective-permute-start(f32[352,128]{1,0:T(8,128)S(1)} %pad_maximum_fusion.1), channel_id=1, source_target_pairs={{1,0},{2,1},{3,2},{4,3},{5,4},{6,5},{7,6},{8,7},{9,8},{10,9},{11,1... | collective-permute-start | bytes 540680 | tf_op jit(solution)/shard_map/ppermute | solution.py:411
  21.7 13.1 %collective-permute-start.4 = (f32[88,128]{1,0:T(8,128)S(1)}, f32[88,128]{1,0:T(8,128)S(1)}, u32[]{:S(2)}, u32[]{:S(2)}) collective-permute-start(f32[88,128]{1,0:T(8,128)S(1)} %shard_map.42), channel_id=1, source_target_pairs={{0,512},{512,0},{1,513},{513,1},{2,514},{514,2},{3,515},{515,3},{4... | collective-permute-start | bytes 135176 | tf_op jit(solution)/shard_map/ppermute | solution.py:429

commit v5 on v4

--- a/solution.py
+++ b/solution.py
@@ -11,7 +11,7 @@
 EPSILON = 1e-06
 INTERPRET = False
 
-SHIFTS = (1.25, 3.25, 8.25, 14.25, 4.25)
+SHIFTS = (0.75, 3.75, 13.25, 9.25, 5.25)
 SCALE = 2.0**24
 FIRST = 6.0 - SHIFTS[0]
 COUNT = ITERS + 1
@@ -437,7 +437,7 @@
         20000000,
         12,
     )(*blocks, side)
-    rows = lax.all_to_all(rows, ("slab", "py"), 0, 0, tiled=True)
+    rows = lax.all_to_all(rows, ("py", "slab"), 0, 0, tiled=True)
     rows = call(rows_kernel, jax.ShapeDtypeStruct((n_z, 128), f32))(rows)
     rows = lax.all_to_all(rows, "pz", 0, 0, tiled=True)
     per_cell = 1.0 / (v.size * n_z * n_xy)

time: 82.2 us -> 82 us (level)
  no operation moved by 1% of the time
where the time goes in v5:
time: 82 us; the launch traced here: 81.6 us
  blocking collectives  42.1 us (51%)
  starting transfers between devices  23.1 us (28%)
  waiting for transfers between devices  9.75 us (12%)
  Pallas kernels  5.05 us (6%)
  local copies, waits for them, and re-layouts  0.87 us (1%)
    all_to_all x1, blocking collectives, shards(): rows = lax.all_to_all(rows, ('py', 'slab'), 0, 0, tiled=True)  23.7 us
    all_to_all x1, blocking collectives, shards(): rows = lax.all_to_all(rows, 'pz', 0, 0, tiled=True)  18.3 us
    ppermute x1, starting transfers between devices, shards(): side = lax.ppermute(side, 'slab', [(0, 1), (1, 0)])  12.2 us
    ppermute x2, starting transfers between devices, exchange(): lax.ppermute(to_next, axis, line(axis, 1))  8.16 us
    ppermute x2, waiting for transfers between devices, exchange(): lax.ppermute(to_previous, axis, line(axis, -1))  7.81 us
    pallas_call x1, Pallas kernels, shards(): call(krylov_kernel, (jax.ShapeDtypeStruct((COUNT, 8, 32, 128), f32), jax....  2.87 us
    ppermute x2, starting transfers between devices, exchange(): lax.ppermute(to_previous, axis, line(axis, -1))  2.72 us
    pallas_call x1, Pallas kernels, shards(): call(functools.partial(lanczos_kernel, per_cell), (jax.ShapeDtypeStruct((...  1.73 us
  transfers between devices with their start and end apart: 5, of which 4 were waited for; matrix products, arithmetic and copies ran while one was open for 0% of the time, Pallas kernels for 0%

profile of v5, /device:TPU:1, one launch (start us, length us, event | category | flops | bytes accessed | tf_op | source)
XLA Modules:
  0.0 81.6 jit_solution(3326920434622861070)
XLA Ops:
  0.6 0.8 %fusion.2 = (f32[8,8,128]{2,1,0:T(8,128)S(1)}, f32[8,8,128]{2,1,0:T(8,128)S(1)}, f32[8,8,128]{2,1,0:T(8,128)S(1)}, f32[8,8,128]{2,1,0:T(8,128)S(1)}) fusion(f32[8,32,128]{2,1,0:T(8,128)} %p.1, f32[8,32,128]{2,1,0:T(8,128)} %v.1), kind=kLoop, calls=%fused_computation.8 | loop fusion | bytes 262144 | tf_op jit(solution)/shard_map/slice | solution.py:418
  1.5 0.0 copy-start
  1.5 4.9 %collective-permute-start = (f32[9,8,128]{2,1,0:T(8,128)S(1)}, f32[9,8,128]{2,1,0:T(8,128)S(1)}, u32[]{:S(2)}, u32[]{:S(2)}) collective-permute-start(f32[9,8,128]{2,1,0:T(8,128)S(1)} %get-tuple-element.6), channel_id=1, source_target_pairs={{0,32},{32,64},{64,96},{96,128},{128,160},{160,192},{192,224},{224... | collective-permute-start | bytes 110600 | tf_op jit(solution)/shard_map/ppermute | solution.py:410
  6.5 0.0 copy-start.1
  6.5 1.4 %collective-permute-start.1 = (f32[9,8,128]{2,1,0:T(8,128)S(1)}, f32[9,8,128]{2,1,0:T(8,128)S(1)}, u32[]{:S(2)}, u32[]{:S(2)}) collective-permute-start(f32[9,8,128]{2,1,0:T(8,128)S(1)} %get-tuple-element.7), channel_id=1, source_target_pairs={{32,0},{64,32},{96,64},{128,96},{160,128},{192,160},{224,192},{256... | collective-permute-start | bytes 110600 | tf_op jit(solution)/shard_map/ppermute | solution.py:411
  7.9 0.0 copy-done
  7.9 0.0 copy-done.1
  8.0 0.0 collective-permute-done.refs_2_.y_low
  8.0 4.0 %collective-permute-done.1.refs_3_.y_high = f32[9,8,128]{2,1,0:T(8,128)S(1)} collective-permute-done((f32[9,8,128]{2,1,0:T(8,128)S(1)}, f32[9,8,128]{2,1,0:T(8,128)S(1)}, u32[]{:S(2)}, u32[]{:S(2)}) %collective-permute-start.1) | collective-permute-done | bytes 36896 | tf_op jit(solution)/shard_map/ppermute | solution.py:411
  12.0 3.2 %collective-permute-start.2 = (f32[352,128]{1,0:T(8,128)S(1)}, f32[352,128]{1,0:T(8,128)S(1)}, u32[]{:S(2)}, u32[]{:S(2)}) collective-permute-start(f32[352,128]{1,0:T(8,128)S(1)} %pad_maximum_fusion), channel_id=1, source_target_pairs={{0,1},{1,2},{2,3},{3,4},{4,5},{5,6},{6,7},{7,8},{8,9},{9,10},{10,1... | collective-permute-start | bytes 540680 | tf_op jit(solution)/shard_map/ppermute | solution.py:410
  15.2 1.3 %collective-permute-start.3 = (f32[352,128]{1,0:T(8,128)S(1)}, f32[352,128]{1,0:T(8,128)S(1)}, u32[]{:S(2)}, u32[]{:S(2)}) collective-permute-start(f32[352,128]{1,0:T(8,128)S(1)} %pad_maximum_fusion.1), channel_id=1, source_target_pairs={{1,0},{2,1},{3,2},{4,3},{5,4},{6,5},{7,6},{8,7},{9,8},{10,9},{11,1... | collective-permute-start | bytes 540680 | tf_op jit(solution)/shard_map/ppermute | solution.py:411
  16.5 1.1 %collective-permute-done.2.refs_4_.z_low = f32[352,128]{1,0:T(8,128)S(1)} collective-permute-done((f32[352,128]{1,0:T(8,128)S(1)}, f32[352,128]{1,0:T(8,128)S(1)}, u32[]{:S(2)}, u32[]{:S(2)}) %collective-permute-start.2) | collective-permute-done | bytes 180256 | tf_op jit(solution)/shard_map/ppermute | solution.py:410
  17.6 3.9 %collective-permute-done.3.refs_5_.z_high = f32[352,128]{1,0:T(8,128)S(1)} collective-permute-done((f32[352,128]{1,0:T(8,128)S(1)}, f32[352,128]{1,0:T(8,128)S(1)}, u32[]{:S(2)}, u32[]{:S(2)}) %collective-permute-start.3) | collective-permute-done | bytes 180256 | tf_op jit(solution)/shard_map/ppermute | solution.py:411
  21.4 0.3 shard_map.42
  21.7 12.2 %collective-permute-start.4 = (f32[88,128]{1,0:T(8,128)S(1)}, f32[88,128]{1,0:T(8,128)S(1)}, u32[]{:S(2)}, u32[]{:S(2)}) collective-permute-start(f32[88,128]{1,0:T(8,128)S(1)} %shard_map.42), channel_id=1, source_target_pairs={{0,512},{512,0},{1,513},{513,1},{2,514},{514,2},{3,515},{515,3},{4... | collective-permute-start | bytes 135176 | tf_op jit(solution)/shard_map/ppermute | solution.py:429
  34.0 0.9 %collective-permute-done.4.side = f32[88,128]{1,0:T(8,128)S(1)} collective-permute-done((f32[88,128]{1,0:T(8,128)S(1)}, f32[88,128]{1,0:T(8,128)S(1)}, u32[]{:S(2)}, u32[]{:S(2)}) %collective-permute-start.4) | collective-permute-done | bytes 45088 | tf_op jit(solution)/shard_map/ppermute | solution.py:429
  34.8 2.9 %shard_map.43 = (f32[6,8,32,128]{3,2,1,0:T(8,128)S(1)}, f32[32,128]{1,0:T(8,128)S(1)}) custom-call(f32[8,32,128]{2,1,0:T(8,128)S(1)} %copy-done, f32[8,32,128]{2,1,0:T(8,128)S(1)} %copy-done.1, f32[9,8,128]{2,1,0:T(8,128)S(1)} %collective-permute-done.refs_2_.y_low, f32[9,8,128]{2,1,0:T(8,128)S(1)} %collective-permute-done.1.refs_3_.y_high, ...), custom_call_target="tpu_custom_call" | custom-call | flops 20000000 | bytes 20000000 | tf_op jit(solution)/shard_map/pallas_call | solution.py:433
  37.7 23.7 %all_to_all.22 = f32[32,1,128]{2,1,0:T(1,128)S(1)} all-to-all(f32[32,1,128]{2,1,0:T(1,128)S(1)} %bitcast.23), channel_id=1, replica_groups=mesh['slab'=2,'py'=16,'pz'=32] {'py','slab'}, dimensions={0} | all-to-all | bytes 32768 | tf_op jit(solution)/shard_map/all_to_all | solution.py:440
  61.4 0.2 shard_map.44
  61.6 18.3 %all_to_all.23 = f32[32,1,128]{2,1,0:T(1,128)S(1)} all-to-all(f32[32,1,128]{2,1,0:T(1,128)S(1)} %bitcast.22), channel_id=1, replica_groups=mesh['slab'=2,'py'=16,'pz'=32] {'pz'}, dimensions={0} | all-to-all | bytes 32768 | tf_op jit(solution)/shard_map/all_to_all | solution.py:442
  79.9 1.7 %shard_map.45 = (f32[6,8,32,128]{3,2,1,0:T(8,128)}, f32[2,5]{1,0:T(2,128)}) custom-call(f32[32,128]{1,0:T(8,128)S(1)} %bitcast.20, f32[6,8,32,128]{3,2,1,0:T(8,128)S(1)} %get-tuple-element.9.basis), custom_call_target="tpu_custom_call" | custom-call | flops 20000000 | bytes 20000000 | tf_op jit(solution)/shard_map/pallas_call | solution.py:444
  (7 shorter events, 0.1 us)
Async XLA Ops:
  1.5 6.4 %copy-start = (f32[8,32,128]{2,1,0:T(8,128)S(1)}, f32[8,32,128]{2,1,0:T(8,128)}, u32[]{:S(2)}) copy-start(f32[8,32,128]{2,1,0:T(8,128)} %v.1) | copy-start | bytes 393220
  1.5 6.5 %collective-permute-start = (f32[9,8,128]{2,1,0:T(8,128)S(1)}, f32[9,8,128]{2,1,0:T(8,128)S(1)}, u32[]{:S(2)}, u32[]{:S(2)}) collective-permute-start(f32[9,8,128]{2,1,0:T(8,128)S(1)} %get-tuple-element.6), channel_id=1, source_target_pairs={{0,32},{32,64},{64,96},{96,128},{128,160},{160,192},{192,224},{224... | collective-permute-start | bytes 110600 | tf_op jit(solution)/shard_map/ppermute | solution.py:410
  6.5 1.5 %copy-start.1 = (f32[8,32,128]{2,1,0:T(8,128)S(1)}, f32[8,32,128]{2,1,0:T(8,128)}, u32[]{:S(2)}) copy-start(f32[8,32,128]{2,1,0:T(8,128)} %p.1) | copy-start | bytes 393220
  6.5 5.5 %collective-permute-start.1 = (f32[9,8,128]{2,1,0:T(8,128)S(1)}, f32[9,8,128]{2,1,0:T(8,128)S(1)}, u32[]{:S(2)}, u32[]{:S(2)}) collective-permute-start(f32[9,8,128]{2,1,0:T(8,128)S(1)} %get-tuple-element.7), channel_id=1, source_target_pairs={{32,0},{64,32},{96,64},{128,96},{160,128},{192,160},{224,192},{256... | collective-permute-start | bytes 110600 | tf_op jit(solution)/shard_map/ppermute | solution.py:411
  12.0 5.6 %collective-permute-start.2 = (f32[352,128]{1,0:T(8,128)S(1)}, f32[352,128]{1,0:T(8,128)S(1)}, u32[]{:S(2)}, u32[]{:S(2)}) collective-permute-start(f32[352,128]{1,0:T(8,128)S(1)} %pad_maximum_fusion), channel_id=1, source_target_pairs={{0,1},{1,2},{2,3},{3,4},{4,5},{5,6},{6,7},{7,8},{8,9},{9,10},{10,1... | collective-permute-start | bytes 540680 | tf_op jit(solution)/shard_map/ppermute | solution.py:410
  15.2 6.2 %collective-permute-start.3 = (f32[352,128]{1,0:T(8,128)S(1)}, f32[352,128]{1,0:T(8,128)S(1)}, u32[]{:S(2)}, u32[]{:S(2)}) collective-permute-start(f32[352,128]{1,0:T(8,128)S(1)} %pad_maximum_fusion.1), channel_id=1, source_target_pairs={{1,0},{2,1},{3,2},{4,3},{5,4},{6,5},{7,6},{8,7},{9,8},{10,9},{11,1... | collective-permute-start | bytes 540680 | tf_op jit(solution)/shard_map/ppermute | solution.py:411
  21.7 13.1 %collective-permute-start.4 = (f32[88,128]{1,0:T(8,128)S(1)}, f32[88,128]{1,0:T(8,128)S(1)}, u32[]{:S(2)}, u32[]{:S(2)}) collective-permute-start(f32[88,128]{1,0:T(8,128)S(1)} %shard_map.42), channel_id=1, source_target_pairs={{0,512},{512,0},{1,513},{513,1},{2,514},{514,2},{3,515},{515,3},{4... | collective-permute-start | bytes 135176 | tf_op jit(solution)/shard_map/ppermute | solution.py:429

commit v6 on v5

--- a/solution.py
+++ b/solution.py
@@ -401,15 +401,17 @@
 def shards(v, p):
     f32 = jnp.float32
 
-    def line(axis, step):
+    def exchange(to_next, to_previous, axis):
         n = lax.axis_size(axis)
-        return [(i, i + step) for i in range(n) if 0 <= i + step < n]
-
-    def exchange(to_next, to_previous, axis):
-        return (
-            lax.ppermute(to_next, axis, line(axis, 1)),
-            lax.ppermute(to_previous, axis, line(axis, -1)),
-        )
+        even = lax.axis_index(axis) % 2 == 0
+
+        def swapped(value, start):
+            pairs = [(i, i + 1) for i in range(start, n - 1, 2)]
+            return lax.ppermute(value, axis, pairs + [(k, i) for i, k in pairs])
+
+        a = swapped(jnp.where(even, to_next, to_previous), 0)
+        b = swapped(jnp.where(even, to_previous, to_next), 1)
+        return jnp.where(even, b, a), jnp.where(even, a, b)
 
     halo = jax.ShapeDtypeStruct((9, 8, 128), f32)
     last, first = slice(24, 32), slice(0, 8)

time: 82 us -> 82.1 us (level)
  waiting for transfers between devices: 9.75 us -> 3.6 us
  starting transfers between devices: 23.1 us -> 26.4 us
  blocking collectives: 42.1 us -> 44.9 us
    ppermute x4, waiting for transfers between devices: 8.9 us -> 2.75 us  [swapped(): return lax.ppermute(value, axis, pairs + [(k, i) for i, k in pairs])]
    ppermute x1, starting transfers between devices: 12.2 us -> 16.9 us  [shards(): side = lax.ppermute(side, 'slab', [(0, 1), (1, 0)])]
    all_to_all x1, blocking collectives: 18.3 us -> 21.9 us  [shards(): rows = lax.all_to_all(rows, 'pz', 0, 0, tiled=True)]
    ppermute x4, starting transfers between devices: 10.9 us -> 9.49 us  [swapped(): return lax.ppermute(value, axis, pairs + [(k, i) for i, k in pairs])]
  transfers between devices with their start and end apart: 5 -> 5, of which waited for: 4 -> 3; matrix products, arithmetic and copies ran while one was open for 0% -> 0% of each run, Pallas kernels for 0% -> 0%
where the time goes in v6:
time: 82.1 us; the launch traced here: 81.7 us
  blocking collectives  44.9 us (55%)
  starting transfers between devices  26.4 us (32%)
  Pallas kernels  5.06 us (6%)
  waiting for transfers between devices  3.6 us (4%)
  local copies, waits for them, and re-layouts  0.93 us (1%)
    all_to_all x1, blocking collectives, shards(): rows = lax.all_to_all(rows, ('py', 'slab'), 0, 0, tiled=True)  23 us
    all_to_all x1, blocking collectives, shards(): rows = lax.all_to_all(rows, 'pz', 0, 0, tiled=True)  21.9 us
    ppermute x1, starting transfers between devices, shards(): side = lax.ppermute(side, 'slab', [(0, 1), (1, 0)])  16.9 us
    ppermute x4, starting transfers between devices, swapped(): return lax.ppermute(value, axis, pairs + [(k, i) for i, k in pairs])  9.49 us
    pallas_call x1, Pallas kernels, shards(): call(krylov_kernel, (jax.ShapeDtypeStruct((COUNT, 8, 32, 128), f32), jax....  2.88 us
    ppermute x4, waiting for transfers between devices, swapped(): return lax.ppermute(value, axis, pairs + [(k, i) for i, k in pairs])  2.75 us
    pallas_call x1, Pallas kernels, shards(): call(functools.partial(lanczos_kernel, per_cell), (jax.ShapeDtypeStruct((...  1.73 us
  transfers between devices with their start and end apart: 5, of which 3 were waited for; matrix products, arithmetic and copies ran while one was open for 0% of the time, Pallas kernels for 0%

profile of v6, /device:TPU:1, one launch (start us, length us, event | category | flops | bytes accessed | tf_op | source)
XLA Modules:
  0.0 81.7 jit_solution(11576518659390309457)
XLA Ops:
  0.6 0.8 %fusion.4 = (f32[8,8,128]{2,1,0:T(8,128)S(1)}, f32[8,8,128]{2,1,0:T(8,128)S(1)}, f32[8,8,128]{2,1,0:T(8,128)S(1)}, f32[8,8,128]{2,1,0:T(8,128)S(1)}) fusion(f32[8,32,128]{2,1,0:T(8,128)} %p.1, f32[8,32,128]{2,1,0:T(8,128)} %v.1), kind=kLoop, calls=%fused_computation.16 | loop fusion | bytes 262144 | tf_op jit(solution)/shard_map/slice | solution.py:420
  1.5 0.0 copy-start
  1.5 4.8 %collective-permute-start.1 = (f32[9,8,128]{2,1,0:T(8,128)S(1)}, f32[9,8,128]{2,1,0:T(8,128)S(1)}, u32[]{:S(2)}, u32[]{:S(2)}) collective-permute-start(f32[9,8,128]{2,1,0:T(8,128)S(1)} %get-tuple-element.24), channel_id=1, source_target_pairs={{0,32},{64,96},{128,160},{192,224},{256,288},{320,352},{384,416},{... | collective-permute-start | bytes 110600 | tf_op jit(solution)/shard_map/ppermute | solution.py:410
  6.4 0.0 copy-start.1
  6.4 0.8 collective-permute-start
  7.2 0.0 copy-done
  7.2 0.1 copy-done.1
  7.3 0.4 collective-permute-done.1
  7.7 0.0 collective-permute-done
  7.8 3.2 %collective-permute-start.3 = (f32[352,128]{1,0:T(8,128)S(1)}, f32[352,128]{1,0:T(8,128)S(1)}, u32[]{:S(2)}, u32[]{:S(2)}) collective-permute-start(f32[352,128]{1,0:T(8,128)S(1)} %get-tuple-element.12), channel_id=1, source_target_pairs={{0,1},{2,3},{4,5},{6,7},{8,9},{10,11},{12,13},{14,15},{16,17},{18,... | collective-permute-start | bytes 540680 | tf_op jit(solution)/shard_map/ppermute | solution.py:410
  11.0 0.7 collective-permute-start.2
  11.7 2.3 %collective-permute-done.3 = f32[352,128]{1,0:T(8,128)S(1)} collective-permute-done((f32[352,128]{1,0:T(8,128)S(1)}, f32[352,128]{1,0:T(8,128)S(1)}, u32[]{:S(2)}, u32[]{:S(2)}) %collective-permute-start.3) | collective-permute-done | bytes 180256 | tf_op jit(solution)/shard_map/ppermute | solution.py:410
  14.0 0.0 collective-permute-done.2
  14.0 0.3 shard_map.42
  14.3 16.9 %collective-permute-start.4 = (f32[88,128]{1,0:T(8,128)S(1)}, f32[88,128]{1,0:T(8,128)S(1)}, u32[]{:S(2)}, u32[]{:S(2)}) collective-permute-start(f32[88,128]{1,0:T(8,128)S(1)} %shard_map.42), channel_id=1, source_target_pairs={{0,512},{512,0},{1,513},{513,1},{2,514},{514,2},{3,515},{515,3},{4... | collective-permute-start | bytes 135176 | tf_op jit(solution)/shard_map/ppermute | solution.py:431
  31.2 0.9 %collective-permute-done.4.side = f32[88,128]{1,0:T(8,128)S(1)} collective-permute-done((f32[88,128]{1,0:T(8,128)S(1)}, f32[88,128]{1,0:T(8,128)S(1)}, u32[]{:S(2)}, u32[]{:S(2)}) %collective-permute-start.4) | collective-permute-done | bytes 45088 | tf_op jit(solution)/shard_map/ppermute | solution.py:431
  32.0 2.9 %shard_map.43 = (f32[6,8,32,128]{3,2,1,0:T(8,128)S(1)}, f32[32,128]{1,0:T(8,128)S(1)}) custom-call(f32[8,32,128]{2,1,0:T(8,128)S(1)} %copy-done, f32[8,32,128]{2,1,0:T(8,128)S(1)} %copy-done.1, f32[9,8,128]{2,1,0:T(8,128)S(1)} %get-tuple-element.23.refs_2_.y_low, f32[9,8,128]{2,1,0:T(8,128)S(1)} %get-tuple-element.22.refs_3_.y_high, ...), custom_call_target="tpu_custom_call" | custom-call | flops 20000000 | bytes 20000000 | tf_op jit(solution)/shard_map/pallas_call | solution.py:435
  34.9 23.0 %all_to_all.22 = f32[32,1,128]{2,1,0:T(1,128)S(1)} all-to-all(f32[32,1,128]{2,1,0:T(1,128)S(1)} %bitcast.23), channel_id=1, replica_groups=mesh['slab'=2,'py'=16,'pz'=32] {'py','slab'}, dimensions={0} | all-to-all | bytes 32768 | tf_op jit(solution)/shard_map/all_to_all | solution.py:442
  57.9 0.2 shard_map.44
  58.0 21.9 %all_to_all.23 = f32[32,1,128]{2,1,0:T(1,128)S(1)} all-to-all(f32[32,1,128]{2,1,0:T(1,128)S(1)} %bitcast.22), channel_id=1, replica_groups=mesh['slab'=2,'py'=16,'pz'=32] {'pz'}, dimensions={0} | all-to-all | bytes 32768 | tf_op jit(solution)/shard_map/all_to_all | solution.py:444
  80.0 1.7 %shard_map.45 = (f32[6,8,32,128]{3,2,1,0:T(8,128)}, f32[2,5]{1,0:T(2,128)}) custom-call(f32[32,128]{1,0:T(8,128)S(1)} %bitcast.20, f32[6,8,32,128]{3,2,1,0:T(8,128)S(1)} %get-tuple-element.9.basis), custom_call_target="tpu_custom_call" | custom-call | flops 20000000 | bytes 20000000 | tf_op jit(solution)/shard_map/pallas_call | solution.py:446
  (9 shorter events, 0.1 us)
Async XLA Ops:
  1.5 5.7 %copy-start = (f32[8,32,128]{2,1,0:T(8,128)S(1)}, f32[8,32,128]{2,1,0:T(8,128)}, u32[]{:S(2)}) copy-start(f32[8,32,128]{2,1,0:T(8,128)} %v.1) | copy-start | bytes 393220
  1.5 6.2 %collective-permute-start.1 = (f32[9,8,128]{2,1,0:T(8,128)S(1)}, f32[9,8,128]{2,1,0:T(8,128)S(1)}, u32[]{:S(2)}, u32[]{:S(2)}) collective-permute-start(f32[9,8,128]{2,1,0:T(8,128)S(1)} %get-tuple-element.24), channel_id=1, source_target_pairs={{0,32},{64,96},{128,160},{192,224},{256,288},{320,352},{384,416},{... | collective-permute-start | bytes 110600 | tf_op jit(solution)/shard_map/ppermute | solution.py:410
  6.4 0.9 %copy-start.1 = (f32[8,32,128]{2,1,0:T(8,128)S(1)}, f32[8,32,128]{2,1,0:T(8,128)}, u32[]{:S(2)}) copy-start(f32[8,32,128]{2,1,0:T(8,128)} %p.1) | copy-start | bytes 393220
  6.4 1.3 %collective-permute-start = (f32[9,8,128]{2,1,0:T(8,128)S(1)}, f32[9,8,128]{2,1,0:T(8,128)S(1)}, u32[]{:S(2)}, u32[]{:S(2)}) collective-permute-start(f32[9,8,128]{2,1,0:T(8,128)S(1)} %get-tuple-element.25), channel_id=1, source_target_pairs={{32,64},{96,128},{160,192},{224,256},{288,320},{352,384},{416,448}... | collective-permute-start | bytes 110600 | tf_op jit(solution)/shard_map/ppermute | solution.py:410
  7.8 6.2 %collective-permute-start.3 = (f32[352,128]{1,0:T(8,128)S(1)}, f32[352,128]{1,0:T(8,128)S(1)}, u32[]{:S(2)}, u32[]{:S(2)}) collective-permute-start(f32[352,128]{1,0:T(8,128)S(1)} %get-tuple-element.12), channel_id=1, source_target_pairs={{0,1},{2,3},{4,5},{6,7},{8,9},{10,11},{12,13},{14,15},{16,17},{18,... | collective-permute-start | bytes 540680 | tf_op jit(solution)/shard_map/ppermute | solution.py:410
  11.0 3.0 %collective-permute-start.2 = (f32[352,128]{1,0:T(8,128)S(1)}, f32[352,128]{1,0:T(8,128)S(1)}, u32[]{:S(2)}, u32[]{:S(2)}) collective-permute-start(f32[352,128]{1,0:T(8,128)S(1)} %get-tuple-element.13), channel_id=1, source_target_pairs={{1,2},{3,4},{5,6},{7,8},{9,10},{11,12},{13,14},{15,16},{17,18},{19... | collective-permute-start | bytes 540680 | tf_op jit(solution)/shard_map/ppermute | solution.py:410
  14.3 17.7 %collective-permute-start.4 = (f32[88,128]{1,0:T(8,128)S(1)}, f32[88,128]{1,0:T(8,128)S(1)}, u32[]{:S(2)}, u32[]{:S(2)}) collective-permute-start(f32[88,128]{1,0:T(8,128)S(1)} %shard_map.42), channel_id=1, source_target_pairs={{0,512},{512,0},{1,513},{513,1},{2,514},{514,2},{3,515},{515,3},{4... | collective-permute-start | bytes 135176 | tf_op jit(solution)/shard_map/ppermute | solution.py:431

commit v7 on v5

--- a/solution.py
+++ b/solution.py
@@ -427,20 +427,20 @@
     blocks = (v, p, y_low, y_high, z_low, z_high)
     side = call(side_kernel, jax.ShapeDtypeStruct((88, 128), f32))(*blocks)
     side = lax.ppermute(side, "slab", [(0, 1), (1, 0)])
-    n_z = lax.axis_size("pz")
-    n_xy = lax.axis_size("slab") * lax.axis_size("py")
+    n_y = lax.axis_size("py")
+    n_zx = lax.axis_size("pz") * lax.axis_size("slab")
     block = [pltpu.VMEM((2, 18, 48, 128), f32)] * 5
     basis, rows = call(
         krylov_kernel,
-        (jax.ShapeDtypeStruct((COUNT, 8, 32, 128), f32), jax.ShapeDtypeStruct((n_xy, 128), f32)),
+        (jax.ShapeDtypeStruct((COUNT, 8, 32, 128), f32), jax.ShapeDtypeStruct((n_y, 128), f32)),
         block + [pltpu.VMEM((8, 32, 128), f32), pltpu.VMEM((2, 16, 48, 128), f32)],
         20000000,
         12,
     )(*blocks, side)
-    rows = lax.all_to_all(rows, ("py", "slab"), 0, 0, tiled=True)
-    rows = call(rows_kernel, jax.ShapeDtypeStruct((n_z, 128), f32))(rows)
-    rows = lax.all_to_all(rows, "pz", 0, 0, tiled=True)
-    per_cell = 1.0 / (v.size * n_z * n_xy)
+    rows = lax.all_to_all(rows, "py", 0, 0, tiled=True)
+    rows = call(rows_kernel, jax.ShapeDtypeStruct((n_zx, 128), f32))(rows)
+    rows = lax.all_to_all(rows, ("pz", "slab"), 0, 0, tiled=True)
+    per_cell = 1.0 / (v.size * n_y * n_zx)
     return call(
         functools.partial(lanczos_kernel, per_cell),
         (

time: 82 us -> 83.7 us (1.021)
  blocking collectives: 42.1 us -> 43.8 us
    all_to_all x2, blocking collectives: 42.1 us -> 43.8 us  [the longest x1 22.6 us: shards(): rows = lax.all_to_all(rows, 'py', 0, 0, tiled=True)]
where the time goes in v7:
time: 83.7 us; the launch traced here: 83.3 us
  blocking collectives  43.8 us (52%)
  starting transfers between devices  23.1 us (28%)
  waiting for transfers between devices  9.75 us (12%)
  Pallas kernels  5.05 us (6%)
  local copies, waits for them, and re-layouts  0.87 us (1%)
    all_to_all x1, blocking collectives, shards(): rows = lax.all_to_all(rows, 'py', 0, 0, tiled=True)  22.6 us
    all_to_all x1, blocking collectives, shards(): rows = lax.all_to_all(rows, ('pz', 'slab'), 0, 0, tiled=True)  21.2 us
    ppermute x1, starting transfers between devices, shards(): side = lax.ppermute(side, 'slab', [(0, 1), (1, 0)])  12.2 us
    ppermute x2, starting transfers between devices, exchange(): lax.ppermute(to_next, axis, line(axis, 1))  8.16 us
    ppermute x2, waiting for transfers between devices, exchange(): lax.ppermute(to_previous, axis, line(axis, -1))  7.81 us
    pallas_call x1, Pallas kernels, shards(): call(krylov_kernel, (jax.ShapeDtypeStruct((COUNT, 8, 32, 128), f32), jax....  2.87 us
    ppermute x2, starting transfers between devices, exchange(): lax.ppermute(to_previous, axis, line(axis, -1))  2.72 us
    pallas_call x1, Pallas kernels, shards(): call(functools.partial(lanczos_kernel, per_cell), (jax.ShapeDtypeStruct((...  1.74 us
  transfers between devices with their start and end apart: 5, of which 4 were waited for; matrix products, arithmetic and copies ran while one was open for 0% of the time, Pallas kernels for 0%

profile of v7, /device:TPU:1, one launch (start us, length us, event | category | flops | bytes accessed | tf_op | source)
XLA Modules:
  0.0 83.3 jit_solution(12158826506033636031)
XLA Ops:
  0.6 0.8 fusion.2
  1.5 0.0 copy-start
  1.5 4.9 %collective-permute-start = (f32[9,8,128]{2,1,0:T(8,128)S(1)}, f32[9,8,128]{2,1,0:T(8,128)S(1)}, u32[]{:S(2)}, u32[]{:S(2)}) collective-permute-start(f32[9,8,128]{2,1,0:T(8,128)S(1)} %get-tuple-element.6), channel_id=1, source_target_pairs={{0,32},{32,64},{64,96},{96,128},{128,160},{160,192},{192,224},{224... | collective-permute-start | bytes 110600 | tf_op jit(solution)/shard_map/ppermute | solution.py:410
  6.5 0.0 copy-start.1
  6.5 1.4 %collective-permute-start.1 = (f32[9,8,128]{2,1,0:T(8,128)S(1)}, f32[9,8,128]{2,1,0:T(8,128)S(1)}, u32[]{:S(2)}, u32[]{:S(2)}) collective-permute-start(f32[9,8,128]{2,1,0:T(8,128)S(1)} %get-tuple-element.7), channel_id=1, source_target_pairs={{32,0},{64,32},{96,64},{128,96},{160,128},{192,160},{224,192},{256... | collective-permute-start | bytes 110600 | tf_op jit(solution)/shard_map/ppermute | solution.py:411
  7.9 0.0 copy-done
  7.9 0.0 copy-done.1
  8.0 0.0 collective-permute-done.refs_2_.y_low
  8.0 4.0 %collective-permute-done.1.refs_3_.y_high = f32[9,8,128]{2,1,0:T(8,128)S(1)} collective-permute-done((f32[9,8,128]{2,1,0:T(8,128)S(1)}, f32[9,8,128]{2,1,0:T(8,128)S(1)}, u32[]{:S(2)}, u32[]{:S(2)}) %collective-permute-start.1) | collective-permute-done | bytes 36896 | tf_op jit(solution)/shard_map/ppermute | solution.py:411
  12.0 3.2 %collective-permute-start.2 = (f32[352,128]{1,0:T(8,128)S(1)}, f32[352,128]{1,0:T(8,128)S(1)}, u32[]{:S(2)}, u32[]{:S(2)}) collective-permute-start(f32[352,128]{1,0:T(8,128)S(1)} %pad_maximum_fusion), channel_id=1, source_target_pairs={{0,1},{1,2},{2,3},{3,4},{4,5},{5,6},{6,7},{7,8},{8,9},{9,10},{10,1... | collective-permute-start | bytes 540680 | tf_op jit(solution)/shard_map/ppermute | solution.py:410
  15.2 1.3 %collective-permute-start.3 = (f32[352,128]{1,0:T(8,128)S(1)}, f32[352,128]{1,0:T(8,128)S(1)}, u32[]{:S(2)}, u32[]{:S(2)}) collective-permute-start(f32[352,128]{1,0:T(8,128)S(1)} %pad_maximum_fusion.1), channel_id=1, source_target_pairs={{1,0},{2,1},{3,2},{4,3},{5,4},{6,5},{7,6},{8,7},{9,8},{10,9},{11,1... | collective-permute-start | bytes 540680 | tf_op jit(solution)/shard_map/ppermute | solution.py:411
  16.5 1.1 %collective-permute-done.2.refs_4_.z_low = f32[352,128]{1,0:T(8,128)S(1)} collective-permute-done((f32[352,128]{1,0:T(8,128)S(1)}, f32[352,128]{1,0:T(8,128)S(1)}, u32[]{:S(2)}, u32[]{:S(2)}) %collective-permute-start.2) | collective-permute-done | bytes 180256 | tf_op jit(solution)/shard_map/ppermute | solution.py:410
  17.6 3.9 %collective-permute-done.3.refs_5_.z_high = f32[352,128]{1,0:T(8,128)S(1)} collective-permute-done((f32[352,128]{1,0:T(8,128)S(1)}, f32[352,128]{1,0:T(8,128)S(1)}, u32[]{:S(2)}, u32[]{:S(2)}) %collective-permute-start.3) | collective-permute-done | bytes 180256 | tf_op jit(solution)/shard_map/ppermute | solution.py:411
  21.4 0.3 shard_map.42
  21.7 12.2 %collective-permute-start.4 = (f32[88,128]{1,0:T(8,128)S(1)}, f32[88,128]{1,0:T(8,128)S(1)}, u32[]{:S(2)}, u32[]{:S(2)}) collective-permute-start(f32[88,128]{1,0:T(8,128)S(1)} %shard_map.42), channel_id=1, source_target_pairs={{0,512},{512,0},{1,513},{513,1},{2,514},{514,2},{3,515},{515,3},{4... | collective-permute-start | bytes 135176 | tf_op jit(solution)/shard_map/ppermute | solution.py:429
  34.0 0.9 %collective-permute-done.4.side = f32[88,128]{1,0:T(8,128)S(1)} collective-permute-done((f32[88,128]{1,0:T(8,128)S(1)}, f32[88,128]{1,0:T(8,128)S(1)}, u32[]{:S(2)}, u32[]{:S(2)}) %collective-permute-start.4) | collective-permute-done | bytes 45088 | tf_op jit(solution)/shard_map/ppermute | solution.py:429
  34.8 2.9 %shard_map.43 = (f32[6,8,32,128]{3,2,1,0:T(8,128)S(1)}, f32[16,128]{1,0:T(8,128)S(1)}) custom-call(f32[8,32,128]{2,1,0:T(8,128)S(1)} %copy-done, f32[8,32,128]{2,1,0:T(8,128)S(1)} %copy-done.1, f32[9,8,128]{2,1,0:T(8,128)S(1)} %collective-permute-done.refs_2_.y_low, f32[9,8,128]{2,1,0:T(8,128)S(1)} %collective-permute-done.1.refs_3_.y_high, ...), custom_call_target="tpu_custom_call" | custom-call | flops 20000000 | bytes 20000000 | tf_op jit(solution)/shard_map/pallas_call | solution.py:433
  37.7 22.6 %all_to_all.22 = f32[16,1,128]{2,1,0:T(1,128)S(1)} all-to-all(f32[16,1,128]{2,1,0:T(1,128)S(1)} %bitcast.23), channel_id=1, replica_groups=mesh['slab'=2,'py'=16,'pz'=32] {'py'}, dimensions={0} | all-to-all | bytes 16384 | tf_op jit(solution)/shard_map/all_to_all | solution.py:440
  60.3 0.2 shard_map.44
  60.4 21.2 %all_to_all.23 = f32[64,1,128]{2,1,0:T(1,128)S(1)} all-to-all(f32[64,1,128]{2,1,0:T(1,128)S(1)} %bitcast.21), channel_id=1, replica_groups=mesh['slab'=2,'py'=16,'pz'=32] {'pz','slab'}, dimensions={0} | all-to-all | bytes 65536 | tf_op jit(solution)/shard_map/all_to_all | solution.py:442
  81.6 1.7 %shard_map.45 = (f32[6,8,32,128]{3,2,1,0:T(8,128)}, f32[2,5]{1,0:T(2,128)}) custom-call(f32[64,128]{1,0:T(8,128)S(1)} %bitcast.20, f32[6,8,32,128]{3,2,1,0:T(8,128)S(1)} %get-tuple-element.9.basis), custom_call_target="tpu_custom_call" | custom-call | flops 20000000 | bytes 20000000 | tf_op jit(solution)/shard_map/pallas_call | solution.py:444
  (7 shorter events, 0.1 us)
Async XLA Ops:
  1.5 6.4 %copy-start = (f32[8,32,128]{2,1,0:T(8,128)S(1)}, f32[8,32,128]{2,1,0:T(8,128)}, u32[]{:S(2)}) copy-start(f32[8,32,128]{2,1,0:T(8,128)} %v.1) | copy-start | bytes 393220
  1.5 6.5 %collective-permute-start = (f32[9,8,128]{2,1,0:T(8,128)S(1)}, f32[9,8,128]{2,1,0:T(8,128)S(1)}, u32[]{:S(2)}, u32[]{:S(2)}) collective-permute-start(f32[9,8,128]{2,1,0:T(8,128)S(1)} %get-tuple-element.6), channel_id=1, source_target_pairs={{0,32},{32,64},{64,96},{96,128},{128,160},{160,192},{192,224},{224... | collective-permute-start | bytes 110600 | tf_op jit(solution)/shard_map/ppermute | solution.py:410
  6.5 1.5 %copy-start.1 = (f32[8,32,128]{2,1,0:T(8,128)S(1)}, f32[8,32,128]{2,1,0:T(8,128)}, u32[]{:S(2)}) copy-start(f32[8,32,128]{2,1,0:T(8,128)} %p.1) | copy-start | bytes 393220
  6.5 5.5 %collective-permute-start.1 = (f32[9,8,128]{2,1,0:T(8,128)S(1)}, f32[9,8,128]{2,1,0:T(8,128)S(1)}, u32[]{:S(2)}, u32[]{:S(2)}) collective-permute-start(f32[9,8,128]{2,1,0:T(8,128)S(1)} %get-tuple-element.7), channel_id=1, source_target_pairs={{32,0},{64,32},{96,64},{128,96},{160,128},{192,160},{224,192},{256... | collective-permute-start | bytes 110600 | tf_op jit(solution)/shard_map/ppermute | solution.py:411
  12.0 5.6 %collective-permute-start.2 = (f32[352,128]{1,0:T(8,128)S(1)}, f32[352,128]{1,0:T(8,128)S(1)}, u32[]{:S(2)}, u32[]{:S(2)}) collective-permute-start(f32[352,128]{1,0:T(8,128)S(1)} %pad_maximum_fusion), channel_id=1, source_target_pairs={{0,1},{1,2},{2,3},{3,4},{4,5},{5,6},{6,7},{7,8},{8,9},{9,10},{10,1... | collective-permute-start | bytes 540680 | tf_op jit(solution)/shard_map/ppermute | solution.py:410
  15.2 6.2 %collective-permute-start.3 = (f32[352,128]{1,0:T(8,128)S(1)}, f32[352,128]{1,0:T(8,128)S(1)}, u32[]{:S(2)}, u32[]{:S(2)}) collective-permute-start(f32[352,128]{1,0:T(8,128)S(1)} %pad_maximum_fusion.1), channel_id=1, source_target_pairs={{1,0},{2,1},{3,2},{4,3},{5,4},{6,5},{7,6},{8,7},{9,8},{10,9},{11,1... | collective-permute-start | bytes 540680 | tf_op jit(solution)/shard_map/ppermute | solution.py:411
  21.7 13.1 %collective-permute-start.4 = (f32[88,128]{1,0:T(8,128)S(1)}, f32[88,128]{1,0:T(8,128)S(1)}, u32[]{:S(2)}, u32[]{:S(2)}) collective-permute-start(f32[88,128]{1,0:T(8,128)S(1)} %shard_map.42), channel_id=1, source_target_pairs={{0,512},{512,0},{1,513},{513,1},{2,514},{514,2},{3,515},{515,3},{4... | collective-permute-start | bytes 135176 | tf_op jit(solution)/shard_map/ppermute | solution.py:429
